TPU v7x, 256 devices: a whole 4x4x8 slice. The times are simulated.
256 devices in a mesh: row: 16 (over z, core), col: 8 (over x_lo, y), head: 2 (over x_hi).
Axes of the slice: x: 4 (x_hi: 2, x_lo: 2; x = x_hi * 2 + x_lo), y: 4, z: 8, core: 2. Of those that a mesh axis runs over, the one named last changes fastest.
Arguments:
- x_lo: float32 [24, 64, 64, 4], P('col', 'row', 'head'), may hold values from -32 to 32
- noise: float32 [24, 64, 64, 16], P('col', 'row'), may hold values from -6 to 6
- t_index: int32 [24], P('col'), may hold values from 0 to 999
- labels: int32 [24], P('col'), may hold values from 0 to 1000
- stale_kv: bfloat16 [2, 24, 32, 32, 1152], P(None, 'col', 'row', None, 'head'), may hold values from -6 to 6
- embed_w: float32 [16, 1152], replicated, may hold values from -1.5 to 1.5
- t_w1: bfloat16 [256, 1152], replicated, may hold values from -0.375 to 0.375
- t_w2: bfloat16 [1152, 1152], P(None, 'row'), may hold values from -0.1875 to 0.1875
- class_table: bfloat16 [1001, 1152], P(None, 'row'), may hold values from -6 to 6
- ada_w: bfloat16 [1152, 6912], P('row'), may hold values from -0.1875 to 0.1875
- qkv_w: bfloat16 [1152, 3, 1152], P(None, None, 'head'), may hold values from -0.1875 to 0.1875
- out_w: bfloat16 [1152, 1152], P('head'), may hold values from -0.1875 to 0.1875
- fc1_w: bfloat16 [1152, 4608], P(None, ('col', 'head')), may hold values from -0.1875 to 0.1875
- fc2_w: bfloat16 [1152, 4608], P(None, ('col', 'head')), may hold values from -0.09375 to 0.09375
Outputs:
- tokens_out: bfloat16 [24, 64, 64, 1152], P('col', 'row', 'head')
All inputs are finite; a program needn't handle non-finite values.
Results may differ from a plain program's by a relative error of at most 0.025.
Values may be sent and summed in bfloat16 or wider, within the bound.
A program may use at most 128 MiB of HBM per device.

v0:
```python
import math

import jax
import jax.numpy as jnp
from jax import lax
from jax.sharding import PartitionSpec as P

HD = 72
TSTEPS = 1000


def copy_for_each(shard, axis):
    devices = lax.axis_size(axis)
    return lax.all_to_all(
        jnp.broadcast_to(shard[None], (devices, *shard.shape)), axis, 0, 0, tiled=True
    )


def laid_out(pieces, dim):
    pieces = jnp.moveaxis(pieces, 0, dim)
    shape = pieces.shape
    return pieces.reshape(*shape[:dim], shape[dim] * shape[dim + 1], *shape[dim + 2 :])


def gathered_copies(shard, axis, dim):
    pieces = copy_for_each(shard, axis)
    return laid_out(pieces, dim)


def padded_2(block, sides, width):
    for axis, dim in sides:
        count = lax.axis_size(axis)
        forward = [(i, i + 1) for i in range(count - 1)]
        backward = [(target, source) for source, target in forward]
        low = lax.ppermute(
            lax.slice_in_dim(block, block.shape[dim] - width, None, axis=dim), axis, forward
        )
        high = lax.ppermute(lax.slice_in_dim(block, 0, width, axis=dim), axis, backward)
        block = jnp.concatenate([low, block, high], axis=dim)
    return block


def taken_together(shard, axis):
    return copy_for_each(shard, axis).sum(axis=0)


def together(arrays, axis):
    line, at, done = (jnp.concatenate([a.reshape(-1) for a in arrays]), 0, [])
    total = taken_together(line, axis)
    for a in arrays:
        done.append(total[at : at + a.size].reshape(a.shape))
        at += a.size
    return tuple(done)


def gathered_total(shard, axis):
    pieces = lax.all_gather(shard, axis).astype(jnp.float32)
    return pieces.sum(axis=0)


def split_up(shard, dim, devices):
    before, after = (shard.shape[:dim], shard.shape[dim + 1 :])
    return jnp.moveaxis(shard.reshape(*before, devices, -1, *after), dim, 0)


def sent_and_summed(shard, axis, dim):
    devices = lax.axis_size(axis)
    pieces = lax.all_to_all(split_up(shard, dim, devices), axis, 0, 0, tiled=True)
    return jnp.sum(pieces.astype(jnp.float32), axis=0)


def turned_gather(arrays, axis, dims):
    turned = [jnp.moveaxis(a, dim, 0) for a, dim in zip(arrays, dims)]
    widths = [t[0].size for t in turned]
    both = jnp.concatenate([t.reshape(-1, w) for t, w in zip(turned, widths)], axis=1)
    out = lax.all_gather(both, axis, axis=0, tiled=True)
    pieces = jnp.split(out, [sum(widths[:k]) for k in range(1, len(widths))], axis=1)
    return tuple(
        (
            jnp.moveaxis(b.reshape(-1, *t.shape[1:]), 0, dim)
            for b, t, dim in zip(pieces, turned, dims)
        )
    )


def upsample_padded(padded):
    upper = padded[:, :-2]
    middle = padded[:, 1:-1]
    lower = padded[:, 2:]
    rows_even = 0.75 * middle + 0.25 * upper
    rows_odd = 0.75 * middle + 0.25 * lower

    def widen(vertical):
        left_side = vertical[:, :, :-2]
        centre = vertical[:, :, 1:-1]
        right_side = vertical[:, :, 2:]
        return jnp.stack(
            [0.75 * centre + 0.25 * left_side, 0.75 * centre + 0.25 * right_side], axis=3
        )

    stacked = jnp.stack([widen(rows_even), widen(rows_odd)], axis=3)
    return stacked.reshape(
        stacked.shape[0], stacked.shape[1], stacked.shape[2], 4 * stacked.shape[-1]
    )


def clamp_edges(padded, axis_dim, at_start, at_end):
    length = padded.shape[axis_dim]
    leading = lax.slice_in_dim(padded, 0, 1, axis=axis_dim)
    second_row = lax.slice_in_dim(padded, 1, 2, axis=axis_dim)
    trailing = lax.slice_in_dim(padded, length - 1, length, axis=axis_dim)
    before_end = lax.slice_in_dim(padded, length - 2, length - 1, axis=axis_dim)
    leading = jnp.where(at_start, second_row, leading)
    trailing = jnp.where(at_end, before_end, trailing)
    return jnp.concatenate(
        [leading, lax.slice_in_dim(padded, 1, length - 1, axis=axis_dim), trailing], axis=axis_dim
    )


def noise_level(t_index):
    step_values = jnp.arange(TSTEPS, dtype=jnp.float32)
    betas = 0.0001 + (0.02 - 0.0001) * step_values / (TSTEPS - 1)
    log_keep = jnp.cumsum(jnp.log(1.0 - betas))
    picked = (jnp.arange(TSTEPS, dtype=jnp.int32)[None, :] == t_index[:, None]).astype(jnp.float32)
    return jnp.exp(jnp.sum(picked * log_keep[None, :], axis=1))


def position_table(row_pos, col_pos, width):
    quarter = width // 4
    omega = 1.0 / 10000.0 ** (jnp.arange(quarter, dtype=jnp.float32) / quarter)
    row_args = row_pos[:, None] * omega[None, :]
    col_args = col_pos[:, None] * omega[None, :]
    row_part = jnp.concatenate([jnp.sin(row_args), jnp.cos(row_args)], axis=1)
    col_part = jnp.concatenate([jnp.sin(col_args), jnp.cos(col_args)], axis=1)
    n_rows = row_pos.shape[0]
    n_cols = col_pos.shape[0]
    return jnp.concatenate(
        [
            jnp.broadcast_to(row_part[:, None, :], (n_rows, n_cols, width // 2)),
            jnp.broadcast_to(col_part[None, :, :], (n_rows, n_cols, width // 2)),
        ],
        axis=2,
    )


def condition(t_index, labels, t_w1, t_w2, class_table):
    half_freq = t_w1.shape[0] // 2
    freqs = jnp.exp(-math.log(10000.0) * jnp.arange(half_freq, dtype=jnp.float32) / half_freq)
    angles = t_index.astype(jnp.float32)[:, None] * freqs[None, :]
    freq_feat = jnp.concatenate([jnp.cos(angles), jnp.sin(angles)], axis=1).astype(jnp.bfloat16)
    t_hidden = jax.nn.silu(jnp.dot(freq_feat, t_w1, preferred_element_type=jnp.float32)).astype(
        jnp.bfloat16
    )
    t_embed = jnp.dot(t_hidden, t_w2, preferred_element_type=jnp.float32)
    onehot = (jnp.arange(class_table.shape[0], dtype=jnp.int32)[None, :] == labels[:, None]).astype(
        jnp.bfloat16
    )
    return t_embed + jnp.dot(onehot, class_table, preferred_element_type=jnp.float32)


def layer_norm(values):
    centre = jnp.mean(values, axis=-1, keepdims=True)
    spread = jnp.mean((values - centre) ** 2, axis=-1, keepdims=True)
    return (values - centre) * lax.rsqrt(spread + 1e-06)


def spread_out(vector):
    return vector[:, None, None, :]


def body(
    x_lo,
    noise,
    t_index,
    labels,
    stale_kv,
    embed_w,
    t_w1,
    t_w2,
    class_table,
    ada_w,
    qkv_w,
    out_w,
    fc1_w,
    fc2_w,
):
    row_index = lax.axis_index("row")
    row_count = lax.axis_size("row")
    head_index = lax.axis_index("head")
    head_count = lax.axis_size("head")
    batch = noise.shape[0]
    tile_rows = noise.shape[1]
    full_cols = noise.shape[2]
    channels = x_lo.shape[3]
    width = embed_w.shape[1]
    abar = noise_level(t_index)
    gathered = gathered_copies(x_lo, "head", 2)
    padded = padded_2(gathered, (("row", 1),), 1)
    padded = clamp_edges(padded, 1, row_index == 0, row_index == row_count - 1)
    padded = jnp.pad(padded, ((0, 0), (0, 0), (1, 1), (0, 0)), mode="edge")
    upsampled = upsample_padded(padded)
    noisy = (
        jnp.sqrt(abar)[:, None, None, None] * upsampled
        + jnp.sqrt(1.0 - abar)[:, None, None, None] * noise
    )
    grouped = noisy.reshape(batch, tile_rows, full_cols, 4, channels)
    total, squares = together(
        (jnp.sum(grouped, axis=(1, 2, 3)), jnp.sum(grouped * grouped, axis=(1, 2, 3))), "row"
    )
    count = 4.0 * tile_rows * row_count * full_cols
    centre = total / count
    spread = squares / count - centre * centre
    normed = (
        (grouped - centre[:, None, None, None, :])
        * lax.rsqrt(spread + 1e-05)[:, None, None, None, :]
    ).reshape(batch, tile_rows, full_cols, 4 * channels)
    row_pos = (row_index * tile_rows + jnp.arange(tile_rows, dtype=jnp.int32)).astype(jnp.float32)
    col_pos = jnp.arange(full_cols, dtype=jnp.float32)
    pos = position_table(row_pos, col_pos, width)
    tokens = (jnp.einsum("bijf,fd->bijd", normed, embed_w) + pos[None]).astype(jnp.bfloat16)
    cond_part = condition(t_index, labels, t_w1, t_w2, class_table)
    cond_act = jax.nn.silu(cond_part).astype(jnp.bfloat16)
    modulation = gathered_total(
        jnp.dot(cond_act, ada_w, preferred_element_type=jnp.float32).astype(jnp.bfloat16), "row"
    ).astype(jnp.float32)
    shift1, scale1, gate1, shift2, scale2, gate2 = jnp.split(modulation, 6, axis=1)
    per_image = tile_rows * full_cols
    flat = tokens.astype(jnp.float32)
    normed1 = (layer_norm(flat) * (1.0 + spread_out(scale1)) + spread_out(shift1)).astype(
        jnp.bfloat16
    )
    local_width = qkv_w.shape[2]
    heads_local = local_width // HD
    qkv = jnp.dot(
        normed1.reshape(batch * per_image, width),
        qkv_w.reshape(width, 3 * local_width),
        preferred_element_type=jnp.float32,
    )
    qkv = qkv.astype(jnp.bfloat16).reshape(batch, per_image, 3, heads_local, HD)
    query = qkv[:, :, 0]
    key_local = qkv[:, :, 1]
    value_local = qkv[:, :, 2]
    scale = 1.0 / math.sqrt(HD)
    fresh = (
        jnp.einsum("bqhd,bkhd->bhqk", query, key_local, preferred_element_type=jnp.float32) * scale
    )
    top_start = jnp.max(fresh, axis=-1)
    probs = jnp.exp(fresh - top_start[..., None])
    mass_start = jnp.sum(probs, axis=-1)
    acc_start = jnp.einsum(
        "bhqk,bkhd->bhqd",
        probs.astype(jnp.bfloat16),
        value_local,
        preferred_element_type=jnp.float32,
    )
    stale_local = stale_kv.reshape(2, batch, -1, local_width)
    per_device = stale_local.shape[2]
    piece = lax.all_gather(stale_local, "row", axis=2, tiled=True)
    key_count = piece.shape[2]
    coarse_key = piece[0].reshape(batch, key_count, heads_local, HD)
    coarse_value = piece[1].reshape(batch, key_count, heads_local, HD)
    scores = jnp.einsum(
        "bqhd,bkhd->bhqk", query, coarse_key, preferred_element_type=jnp.float32
    ) * scale + math.log(4.0)
    key_device = jnp.arange(key_count, dtype=jnp.int32) // per_device
    scores = jnp.where((key_device == row_index)[None, None, None, :], jnp.float32(-1e30), scores)
    new_top = jnp.maximum(top_start, jnp.max(scores, axis=-1))
    shrink = jnp.exp(top_start - new_top)
    weights = jnp.exp(scores - new_top[..., None])
    new_mass = mass_start * shrink + jnp.sum(weights, axis=-1)
    new_acc = acc_start * shrink[..., None] + jnp.einsum(
        "bhqk,bkhd->bhqd",
        weights.astype(jnp.bfloat16),
        coarse_value,
        preferred_element_type=jnp.float32,
    )
    attended = (new_acc / new_mass[..., None]).astype(jnp.bfloat16)
    attended = attended.transpose(0, 2, 1, 3).reshape(batch * per_image, local_width)
    attn_part = jnp.dot(attended, out_w, preferred_element_type=jnp.float32).reshape(
        batch, tile_rows, full_cols, width
    )
    half_cols = full_cols // head_count
    col_start = head_index * half_cols
    projected = sent_and_summed(attn_part.astype(jnp.bfloat16), "head", 2)
    flat_half = lax.dynamic_slice_in_dim(flat, col_start, half_cols, 2)
    mid_half = (flat_half + spread_out(gate1) * projected).astype(jnp.bfloat16)
    normed2_half = (
        layer_norm(mid_half.astype(jnp.float32)) * (1.0 + spread_out(scale2)) + spread_out(shift2)
    ).astype(jnp.bfloat16)
    normed2 = gathered_copies(normed2_half, "head", 2)
    normed2_rows = normed2.reshape(batch * per_image, width)
    up_piece, down_piece = turned_gather((fc1_w, fc2_w), "col", (1, 1))
    hidden = jax.nn.gelu(
        jnp.dot(normed2_rows, up_piece, preferred_element_type=jnp.float32), approximate=True
    ).astype(jnp.bfloat16)
    mlp_part = lax.dot_general(
        hidden, down_piece, (((1,), (1,)), ((), ())), preferred_element_type=jnp.float32
    )
    mlp_term = sent_and_summed(
        mlp_part.reshape(batch, tile_rows, full_cols, width).astype(jnp.bfloat16), "head", 2
    )
    tokens_out = (mid_half.astype(jnp.float32) + spread_out(gate2) * mlp_term).astype(jnp.bfloat16)
    return tokens_out


def solution(mesh):
    placed = (
        P("col", "row", "head", None),
        P("col", "row", None, None),
        P("col"),
        P("col"),
        P(None, "col", "row", None, "head"),
        P(),
        P(),
        P(None, "row"),
        P(None, "row"),
        P("row", None),
        P(None, None, "head"),
        P("head", None),
        P(None, ("col", "head")),
        P(None, ("col", "head")),
    )
    return jax.shard_map(
        body, mesh=mesh, in_specs=placed, out_specs=P("col", "row", "head", None), check_vma=False
    )
```

profile of v0, /device:TPU:1, one launch (start us, length us, event | category | flops | bytes accessed | tf_op | source)
XLA Modules:
  0.0 293.6 jit_solution(5199491474967571187)
XLA Ops:
  6.6 2.5 copy.89
  10.6 4.8 %all-to-all-start = ((f32[2,1,1536]{2,1,0:T(1,128)}), f32[2,1,1536]{2,1,0:T(1,128)S(1)}, u32[]{:S(2)}, u32[]{:S(2)}) async-start(f32[2,1,1536]{2,1,0:T(1,128)} %reshape.224), calls=%async_computation | async-start | bytes 24576 | tf_op jit(solution)/shard_map/all_to_all | solution.py:14
  15.4 2.5 pad_maximum_fusion
  19.9 27.8 %all-gather.1 = bf16[16,3,6912]{2,1,0:T(4,128)(2,1)S(1)} all-gather(bf16[1,3,6912]{2,1,0:T(4,128)(2,1)S(1)} %fusion.6), channel_id=2, replica_groups=mesh['row'=16,'col'=8,'head'=2] {'row'}, dimensions={0}, use_global_device_ids=true | all-gather | bytes 705024 | tf_op jit(solution)/shard_map/all_gather | solution.py:57
  50.3 1.9 collective-permute-start
  52.2 2.4 collective-permute-start.1
  54.7 2.9 collective-permute-done.1
  59.3 6.1 %all-to-all-start.1 = ((f32[16,1,24]{2,1,0:T(1,128)}), f32[16,1,24]{2,1,0:T(1,128)S(1)}, u32[]{:S(2)}, u32[]{:S(2)}) async-start(f32[16,1,24]{2,1,0:T(1,128)} %broadcast_in_dim.19), calls=%async_computation.1 | async-start | bytes 16384 | tf_op jit(solution)/shard_map/all_to_all | solution.py:14
  65.4 7.0 %all-to-all-done.1 = f32[16,1,24]{2,1,0:T(1,128)S(1)} async-done(((f32[16,1,24]{2,1,0:T(1,128)}), f32[16,1,24]{2,1,0:T(1,128)S(1)}, u32[]{:S(2)}, u32[]{:S(2)}) %all-to-all-start.1) | async-done | bytes 1568 | tf_op jit(solution)/shard_map/all_to_all | solution.py:14
  74.3 1.3 add_convert_fusion
  75.6 1.6 copy-done.13
  77.2 5.0 %convolution_convert_fusion.2 = bf16[768,1728]{0,1:T(8,128)(2,1)} fusion(bf16[768,1152]{1,0:T(8,128)(2,1)S(1)} %bitcast.127, bf16[1152,1728]{0,1:T(8,128)(2,1)S(1)} %bitcast.133), kind=kOutput, calls=%fused_computation.34 | convolution fusion | flops 3058974720 | bytes 8404992 | tf_op jit(solution)/shard_map/dot_general | solution.py:234
  82.1 7.0 %reshape.211 = bf16[3,256,3,8,72]{1,0,4,3,2:T(4,128)(2,1)} reshape(bf16[768,1728]{0,1:T(8,128)(2,1)} %convolution_convert_fusion.2) | data formatting | bytes 5308416 | tf_op jit(solution)/shard_map/reshape | solution.py:239
  89.1 3.3 %fusion.106 = (bf16[3,256,1,8,72]{1,0,4,3,2:T(4,128)(2,1)S(1)}, bf16[3,256,1,8,72]{1,0,4,3,2:T(4,128)(2,1)S(1)}, bf16[3,256,1,8,72]{1,0,4,3,2:T(4,128)(2,1)S(1)}) fusion(bf16[3,256,3,8,72]{1,0,4,3,2:T(4,128)(2,1)} %reshape.211), kind=kLoop, calls=%fused_computation.170 | loop fusion | bytes 5308416 | tf_op jit(solution)/shard_map/slice | solution.py:242
  94.6 2.4 fusion.28
  97.0 16.6 %fusion.105 = (bf16[1,3,1024,576]{3,0,1,2:T(2,128)(2,1)}, bf16[1,3,1024,576]{3,0,1,2:T(2,128)(2,1)}) fusion(bf16[2,3,1024,576]{3,0,1,2:T(2,128)(2,1)} %all-gather.5.cloned.1.call-done), kind=kLoop, calls=%fused_computation.169 | loop fusion | bytes 14155776 | tf_op jit(solution)/shard_map/slice | solution.py:260
  113.5 15.9 %copy.91 = bf16[1,3,1024,576]{2,3,1,0:T(8,128)(2,1)} copy(bf16[1,3,1024,576]{3,0,1,2:T(2,128)(2,1)} %get-tuple-element.13) | data formatting | bytes 7077888 | tf_op jit(solution)/shard_map/slice | solution.py:261
  129.5 15.9 %copy.90 = bf16[1,3,1024,576]{2,3,1,0:T(8,128)(2,1)} copy(bf16[1,3,1024,576]{3,0,1,2:T(2,128)(2,1)} %get-tuple-element.12) | data formatting | bytes 7077888 | tf_op jit(solution)/shard_map/slice | solution.py:260
  145.3 14.0 %fusion.2 = (f32[3,8,256]{2,1,0:T(8,128)S(1)}, f32[3,8,256,1024]{3,2,1,0:T(8,128)}) fusion(pred[1024]{0:T(1024)(128)(4,1)S(1)} %fusion.72, bf16[3,1024,8,72]{1,3,2,0:T(8,128)(2,1)} %bitcast.123, bf16[3,256,1,8,72]{1,0,4,3,2:T(4,128)(2,1)S(1)} %get-tuple-element.16), kind=kOutput, calls=%fused_computation.4 | convolution fusion | flops 931129344 | bytes 29615104 | tf_op jit(solution)/shard_map/bqhd,bkhd->bhqk/dot_general | solution.py:262
  159.3 12.5 %fusion = f32[3,8,256]{2,1,0:T(8,128)S(1)} fusion(f32[3,8,256,1024]{3,2,1,0:T(8,128)} %get-tuple-element.50, f32[3,8,256]{2,1,0:T(8,128)S(1)} %max.18, pred[1024]{0:T(1024)(128)(4,1)S(1)} %fusion.72), kind=kLoop, calls=%fused_computation.2 | loop fusion | flops 31451136 | bytes 25216000 | tf_op jit(solution)/shard_map/reduce_sum | solution.py:270
  171.9 12.3 %fusion.41 = bf16[3,256,8,72]{1,3,2,0:T(8,128)(2,1)} fusion(f32[3,8,256,72]{2,3,1,0:T(8,128)S(1)} %copy-done.4, bf16[3,1024,8,72]{1,3,2,0:T(8,128)(2,1)S(1)} %bitcast.122, f32[3,8,256,1024]{3,2,1,0:T(8,128)} %get-tuple-element.50, f32[3,8,256]{2,1,0:T(8,128)S(1)} %max.18, pred[1024]{0:T(1024)(128)(4,1)S(1)} %fusion.72, ...), kind=kOutput, calls=%fused_computation.52 | convolution fusion | flops 939196416 | bytes 31433728 | tf_op jit(solution)/shard_map/bhqk,bkhd->bhqd/dot_general | solution.py:271
  184.2 3.0 %reshape.222 = bf16[3,4,64,576]{2,1,3,0:T(4,128)(2,1)S(1)} reshape(bf16[3,256,8,72]{1,3,2,0:T(8,128)(2,1)} %fusion.41) | data formatting | bytes 1769472 | tf_op jit(solution)/shard_map/dot_general | solution.py:279
  187.2 1.8 convolution_convert_fusion.1
  188.9 1.4 copy.121
  190.3 4.5 %all-to-all-start.2 = ((bf16[2,3,4,32,1152]{4,3,2,1,0:T(8,128)(2,1)}), bf16[2,3,4,32,1152]{4,3,2,1,0:T(8,128)(2,1)S(1)}, u32[]{:S(2)}, u32[]{:S(2)}) async-start(bf16[2,3,4,32,1152]{4,3,2,1,0:T(8,128)(2,1)} %bitcast.119), calls=%async_computation.2 | async-start | bytes 3538944 | tf_op jit(solution)/shard_map/all_to_all | solution.py:68
  194.9 22.0 %all-to-all-done.2 = bf16[2,3,4,32,1152]{4,3,2,1,0:T(8,128)(2,1)S(1)} async-done(((bf16[2,3,4,32,1152]{4,3,2,1,0:T(8,128)(2,1)}), bf16[2,3,4,32,1152]{4,3,2,1,0:T(8,128)(2,1)S(1)}, u32[]{:S(2)}, u32[]{:S(2)}) %all-to-all-start.2) | async-done | bytes 1769504 | tf_op jit(solution)/shard_map/all_to_all | solution.py:68
  217.2 1.7 copy-done.2
  220.3 23.7 %all_to_all.26 = bf16[2,3,4,32,1152]{4,3,2,1,0:T(8,128)(2,1)S(1)} all-to-all(bf16[2,3,4,32,1152]{4,3,2,1,0:T(8,128)(2,1)S(1)} %broadcast_in_dim.24), channel_id=1, replica_groups=mesh['row'=16,'col'=8,'head'=2] {'head'}, dimensions={0} | all-to-all | bytes 3538944 | tf_op jit(solution)/shard_map/all_to_all | solution.py:14
  244.0 1.4 copy.94
  245.4 15.3 %fusion.25 = bf16[768,1152]{1,0:T(8,128)(2,1)} fusion(bf16[2304,2304]{1,0:T(8,128)(2,1)} %all-gather.7.cloned.1.call-done, bf16[768,1152]{1,0:T(8,128)(2,1)} %bitcast.125), kind=kOutput, calls=%fused_computation.35 | convolution fusion | flops 8170536960 | bytes 14155776 | tf_op jit(solution)/shard_map/dot_general | solution.py:296
  260.7 1.7 copy.120
  262.4 22.9 %all_to_all.27 = bf16[2,3,4,32,1152]{4,3,2,1,0:T(8,128)(2,1)S(1)} all-to-all(bf16[2,3,4,32,1152]{4,3,2,1,0:T(8,128)(2,1)S(1)} %bitcast.121), channel_id=1, replica_groups=mesh['row'=16,'col'=8,'head'=2] {'head'}, dimensions={0} | all-to-all | bytes 3538944 | tf_op jit(solution)/shard_map/all_to_all | solution.py:68
  (114 shorter events, 14.8 us)
Async XLA Ops:
  6.5 180.6 %copy-start = (bf16[576,1152]{1,0:T(8,128)(2,1)S(1)}, bf16[576,1152]{1,0:T(8,128)(2,1)}, u32[]{:S(2)}) copy-start(bf16[576,1152]{1,0:T(8,128)(2,1)} %param.25) | copy-start | bytes 3981316
  6.5 12.4 %copy-start.12 = (s32[3]{0:T(128)S(1)}, s32[3]{0:T(128)}, u32[]{:S(2)}) copy-start(s32[3]{0:T(128)} %param.16) | copy-start | bytes 40
  6.5 12.5 %copy-start.7 = (bf16[1152,72]{0,1:T(8,128)(2,1)S(1)}, bf16[1152,72]{0,1:T(8,128)(2,1)}, u32[]{:S(2)}) copy-start(bf16[1152,72]{0,1:T(8,128)(2,1)} %param.21) | copy-start | bytes 497668
  6.5 12.5 %copy-start.6 = (bf16[256,1152]{1,0:T(8,128)(2,1)S(1)}, bf16[256,1152]{1,0:T(8,128)(2,1)}, u32[]{:S(2)}) copy-start(bf16[256,1152]{1,0:T(8,128)(2,1)} %param.20) | copy-start | bytes 1769476
  6.5 12.9 %copy-start.5 = (bf16[72,6912]{1,0:T(8,128)(2,1)S(1)}, bf16[72,6912]{1,0:T(8,128)(2,1)}, u32[]{:S(2)}) copy-start(bf16[72,6912]{1,0:T(8,128)(2,1)} %param.23) | copy-start | bytes 2985988
  6.5 12.9 %copy-start.8 = (bf16[1001,72]{0,1:T(8,128)(2,1)S(1)}, bf16[1001,72]{0,1:T(8,128)(2,1)}, u32[]{:S(2)}) copy-start(bf16[1001,72]{0,1:T(8,128)(2,1)} %param.22) | copy-start | bytes 432436
  6.6 12.9 %copy-start.11 = (s32[3]{0:T(128)S(1)}, s32[3]{0:T(128)}, u32[]{:S(2)}) copy-start(s32[3]{0:T(128)} %param.17) | copy-start | bytes 40
  6.6 90.4 %all-gather.5.cloned.1.call-start = ((), (), s32[]{:S(2)}) async-start(), calls=%async_computation.5 | async-start | bytes 8355840 | tf_op jit(solution)/shard_map/all_gather | solution.py:258
  10.6 38.4 %all-to-all-start = ((f32[2,1,1536]{2,1,0:T(1,128)}), f32[2,1,1536]{2,1,0:T(1,128)S(1)}, u32[]{:S(2)}, u32[]{:S(2)}) async-start(f32[2,1,1536]{2,1,0:T(1,128)} %reshape.224), calls=%async_computation | async-start | bytes 24576 | tf_op jit(solution)/shard_map/all_to_all | solution.py:14
  15.4 230.0 %all-gather.7.cloned.1.call-start = ((), (), s32[]{:S(2)}) async-start(), calls=%async_computation.6 | async-start | bytes 11943936 | tf_op jit(solution)/shard_map/all_gather | solution.py:76
  47.8 10.3 %copy-start.9 = (f32[3,4,64,16]{2,3,1,0:T(8,128)S(1)}, f32[3,4,64,16]{2,3,1,0:T(8,128)}, u32[]{:S(2)}) copy-start(f32[3,4,64,16]{2,3,1,0:T(8,128)} %param.15) | copy-start | bytes 147460
  48.1 24.8 %copy-start.10 = (f32[16,1152]{1,0:T(8,128)S(1)}, f32[16,1152]{1,0:T(8,128)}, u32[]{:S(2)}) copy-start(f32[16,1152]{1,0:T(8,128)} %param.19) | copy-start | bytes 221188
  50.3 4.4 %collective-permute-start = (f32[3,1,64,4]{2,3,1,0:T(4,128)S(1)}, f32[3,1,64,4]{2,3,1,0:T(4,128)S(1)}, u32[]{:S(2)}, u32[]{:S(2)}) collective-permute-start(f32[3,1,64,4]{2,3,1,0:T(4,128)S(1)} %get-tuple-element.33), channel_id=1, source_target_pairs={{0,16},{16,32},{32,48},{48,64},{64,80},{80,96},{96,112},{112,128},... | collective-permute-start | bytes 9224 | tf_op jit(solution)/shard_map/ppermute | solution.py:35
  52.2 5.3 %collective-permute-start.1 = (f32[3,1,64,4]{2,3,1,0:T(4,128)S(1)}, f32[3,1,64,4]{2,3,1,0:T(4,128)S(1)}, u32[]{:S(2)}, u32[]{:S(2)}) collective-permute-start(f32[3,1,64,4]{2,3,1,0:T(4,128)S(1)} %get-tuple-element.34), channel_id=1, source_target_pairs={{16,0},{32,16},{48,32},{64,48},{80,64},{96,80},{112,96},{128,112},... | collective-permute-start | bytes 9224 | tf_op jit(solution)/shard_map/ppermute | solution.py:38
  59.3 13.2 %all-to-all-start.1 = ((f32[16,1,24]{2,1,0:T(1,128)}), f32[16,1,24]{2,1,0:T(1,128)S(1)}, u32[]{:S(2)}, u32[]{:S(2)}) async-start(f32[16,1,24]{2,1,0:T(1,128)} %broadcast_in_dim.19), calls=%async_computation.1 | async-start | bytes 16384 | tf_op jit(solution)/shard_map/all_to_all | solution.py:14
  73.8 1.8 copy-start.1
  74.3 2.9 copy-start.13
  159.3 12.6 %copy-start.3 = (bf16[1,3,1024,576]{2,3,1,0:T(8,128)(2,1)S(1)}, bf16[1,3,1024,576]{2,3,1,0:T(8,128)(2,1)}, u32[]{:S(2)}) copy-start(bf16[1,3,1024,576]{2,3,1,0:T(8,128)(2,1)} %copy.91) | copy-start | bytes 10616836
  159.3 12.6 %copy-start.4 = (f32[3,8,256,72]{2,3,1,0:T(8,128)S(1)}, f32[3,8,256,72]{2,3,1,0:T(8,128)}, u32[]{:S(2)}) copy-start(f32[3,8,256,72]{2,3,1,0:T(8,128)} %fusion.28) | copy-start | bytes 5308420
  190.3 26.6 %all-to-all-start.2 = ((bf16[2,3,4,32,1152]{4,3,2,1,0:T(8,128)(2,1)}), bf16[2,3,4,32,1152]{4,3,2,1,0:T(8,128)(2,1)S(1)}, u32[]{:S(2)}, u32[]{:S(2)}) async-start(bf16[2,3,4,32,1152]{4,3,2,1,0:T(8,128)(2,1)} %bitcast.119), calls=%async_computation.2 | async-start | bytes 3538944 | tf_op jit(solution)/shard_map/all_to_all | solution.py:68
  216.9 2.0 copy-start.2
Sparse Core Ops, SparseCore 0:
  9.2 62.3 all-gather.4
  73.4 113.2 all-gather.6
where the time goes:
time: 297 us; the launch traced here: 294 us
  local copies, waits for them, and re-layouts  75.8 us (26%)
  blocking collectives  74.4 us (25%)
  matrix products  53.4 us (18%)
  waiting for transfers between devices  32 us (11%)
  other arithmetic  24.2 us (8%)
  starting transfers between devices  19.8 us (7%)
  between operations  13.9 us (5%)
    slice x2, local copies, waits for them, and re-layouts, body(): coarse_key = piece[0].reshape(batch, key_count, heads_local, HD)  32.4 us
    all_gather x1, blocking collectives, gathered_total(): pieces = lax.all_gather(shard, axis).astype(jnp.float32)  27.8 us
    all_to_all x1, blocking collectives, copy_for_each(): lax.all_to_all(jnp.broadcast_to(shard[None], (devices, *shard.shape)), ax...  23.7 us
    all_to_all x1, blocking collectives, sent_and_summed(): lax.all_to_all(split_up(shard, dim, devices), axis, 0, 0, tiled=True)  22.9 us
    all_to_all x1, waiting for transfers between devices, sent_and_summed(): lax.all_to_all(split_up(shard, dim, devices), axis, 0, 0, tiled=True)  22 us
    slice x1, local copies, waits for them, and re-layouts, body(): coarse_value = piece[1].reshape(batch, key_count, heads_local, HD)  15.9 us
    dot_general x1, matrix products, body(): lax.dot_general(hidden, down_piece, (((1,), (1,)), ((), ())), preferred_e...  15.3 us
    dot_general x1, matrix products, body(): jnp.einsum('bqhd,bkhd->bhqk', query, coarse_key, preferred_element_type=j...  14 us
  transfers between devices with their start and end apart: 7, of which 3 were waited for; matrix products, arithmetic and copies ran while one was open for 44% of the time, Pallas kernels for 0%

commit v1 on v0

--- a/solution.py
+++ b/solution.py
@@ -3,6 +3,8 @@
 import jax
 import jax.numpy as jnp
 from jax import lax
+from jax.experimental import pallas as pl
+from jax.experimental.pallas import tpu as pltpu
 from jax.sharding import PartitionSpec as P
 
 HD = 72
@@ -166,6 +168,338 @@
 
 def spread_out(vector):
     return vector[:, None, None, :]
+
+
+def fused_block(tok, mod, stale, wqkv, ow, fc1, fc2):
+    D = 1152
+    L2E = 1.4426950408889634
+    QS = L2E / math.sqrt(HD)
+    bf, f32 = jnp.bfloat16, jnp.float32
+    NKEY = 256 + 15 * 64
+    HID = 4608
+    names = []
+
+    def kernel(
+        tok_h, mod_h, stale_h, wqkv_h, ow_h, fc1_h, fc2_h, out_ref,
+        tok, mod, wq, kvb, wb, owb, qb, att, attr, n2, mid, acc, send, recv, local,
+    ):
+        row, col, head = lax.axis_index("row"), lax.axis_index("col"), lax.axis_index("head")
+        z, core = row // 2, row % 2
+        x, y = head * 2 + col // 4, col % 4
+
+        def at(x_, y_, z_, core_):
+            return (z_ * 2 + core_, (x_ % 2) * 4 + y_, x_ // 2)
+
+        peers = {
+            "sib": at(x, y, z, 1 - core),
+            "zp": at(x, y, (z + 1) % 8, core),
+            "zm": at(x, y, (z + 7) % 8, core),
+            "ap": at((x + core) % 4, (y + 1 - core) % 4, z, core),
+            "am": at((x + 4 - core) % 4, (y + 3 + core) % 4, z, core),
+            "bp": at((x + 1 - core) % 4, (y + core) % 4, z, core),
+            "bm": at((x + 3 + core) % 4, (y + 4 - core) % 4, z, core),
+            "far": at((x + 2) % 4, y, z, core),
+        }
+        other = at(3 - x, y, z, core)
+
+        copies = {}
+        order = {"n": 0}
+
+        def remote(name, src, dst, peer):
+            k = order["n"]
+            order["n"] = k + 1
+            c = pltpu.make_async_remote_copy(
+                src_ref=src, dst_ref=dst, send_sem=send.at[k], recv_sem=recv.at[k],
+                device_id=peer, device_id_type=pl.DeviceIdType.MESH,
+            )
+            copies[name] = c
+            return c
+
+        def go(name):
+            copies[name].start()
+
+        def got(name):
+            copies[name].wait_recv()
+
+        loads = []
+
+        def load(src, dst):
+            c = pltpu.make_async_copy(src, dst, local.at[len(loads)])
+            loads.append(c)
+            c.start()
+            return c
+
+        half_own = pl.ds(pl.multiple_of(core * 144, 16), 144)
+
+        def blk(group, chain, j, part=None):
+            base = (group * 8 + chain * 4 + j) * 144
+            lo, n = {None: (0, 144), 0: (0, 80), 1: (80, 64)}[part]
+            return wb.at[:, pl.ds(base + lo, n), :]
+
+        def ring(tag, first, sides, own, place):
+            p, m = sides
+            remote(tag + "1", own(None), place(1, None), p)
+            remote(tag + "2", own(None), place(2, None), m)
+            remote(tag + "3a", place(1, 0), place(3, 0), p)
+            remote(tag + "3b", place(2, 1), place(3, 1), m)
+
+        ap, am, bp, bm = peers["ap"], peers["am"], peers["bp"], peers["bm"]
+        ring("A", 0, (ap, am), lambda part: blk(0, 0, 0, part), lambda g, part: blk(g, 0, 0, part))
+        for g in range(4):
+            ring(
+                f"B{g}", g, (bp, bm), lambda part, g=g: blk(g, 0, 0, part),
+                lambda j, part, g=g: blk(g, 0, j, part),
+            )
+            src = wb.at[:, pl.ds(g * 8 * 144, 576), :]
+            dst = wb.at[:, pl.ds((g * 8 + 4) * 144, 576), :]
+            remote(f"S{g}", src, dst, peers["sib"])
+
+        def slot(b, s, lo=0, n=64):
+            return kvb.at[b, pl.ds(256 + s * 64 + lo, n), :]
+
+        for b in range(3):
+            own = stale_h.at[b]
+            zp, zm = peers["zp"], peers["zm"]
+            remote(f"R1_{b}", own, slot(b, 0), zp)
+            remote(f"L1_{b}", own, slot(b, 3), zm)
+            for d in (1, 2):
+                remote(f"R{d + 1}_{b}", slot(b, d - 1), slot(b, d), zp)
+                remote(f"L{d + 1}_{b}", slot(b, 3 + d - 1), slot(b, 3 + d), zm)
+            remote(f"R4_{b}", slot(b, 2, 0, 32), slot(b, 6, 0, 32), zp)
+            remote(f"L4_{b}", slot(b, 5, 32, 32), slot(b, 6, 32, 32), zm)
+            remote(f"C0_{b}", own, slot(b, 7), peers["sib"])
+            remote(
+                f"C1_{b}", kvb.at[b, pl.ds(256, 448), :], kvb.at[b, pl.ds(256 + 512, 448), :],
+                peers["sib"],
+            )
+            remote(
+                f"X{b}", att.at[b, pl.ds(pl.multiple_of((1 - head) * 128, 128), 128), :],
+                attr.at[b], peers["far"],
+            )
+        ow_own = pl.ds(pl.multiple_of(core * 288, 16), 288)
+        ow_far = pl.ds(pl.multiple_of(704 + core * 288, 16), 288)
+        remote("O", ow_h.at[ow_own, :], owb.at[ow_far, :], other)
+        remote("OS", owb.at[ow_far, :], owb.at[ow_far, :], peers["sib"])
+
+        c_w1 = load(fc1_h.at[half_own, :], wb.at[0, pl.ds(0, 144), :])
+        c_w2 = load(fc2_h.at[half_own, :], wb.at[1, pl.ds(0, 144), :])
+        c_tok = load(tok_h, tok)
+        c_mod = load(mod_h, mod)
+        c_wq = load(wqkv_h, wq)
+        c_ow = load(ow_h, owb.at[pl.ds(64, 576), :])
+        barrier = pltpu.get_barrier_semaphore()
+        for peer in peers.values():
+            pl.semaphore_signal(barrier, inc=1, device_id=peer, device_id_type=pl.DeviceIdType.MESH)
+        pl.semaphore_wait(barrier, len(peers))
+        for b in range(3):
+            go(f"R1_{b}")
+            go(f"L1_{b}")
+        c_w1.wait()
+        c_w2.wait()
+        for n in ("A1", "A2", "B01", "B02"):
+            go(n)
+        for b in range(3):
+            go(f"C0_{b}")
+        go("O")
+
+        owb[pl.ds(0, 64), :] = jnp.zeros((64, D), bf)
+        owb[pl.ds(640, 64), :] = jnp.zeros((64, D), bf)
+        att[...] = jnp.zeros_like(att)
+        c_tok.wait()
+        c_mod.wait()
+        c_wq.wait()
+
+        def norm(v):
+            centre = jnp.mean(v, axis=-1, keepdims=True)
+            v = v - centre
+            spread = jnp.mean(v * v, axis=-1, keepdims=True)
+            return v * lax.rsqrt(spread + 1e-06)
+
+        def modrow(b, k):
+            return mod[pl.ds(b * 6 + k, 1), :]
+
+        NT = (((1,), (1,)), ((), ()))
+
+        def qkv(b):
+            n1 = (
+                norm(tok[pl.ds(b * 256, 256), :].astype(f32)) * (1.0 + modrow(b, 1)) + modrow(b, 0)
+            ).astype(bf)
+            q = lax.dot_general(n1, wq[pl.ds(0, 576), :], NT, preferred_element_type=f32)
+            qb[b, :, pl.ds(0, 576)] = (q * QS).astype(bf)
+            kv = lax.dot_general(n1, wq[pl.ds(576, 1152), :], NT, preferred_element_type=f32)
+            kvb[b, pl.ds(0, 256), :] = kv.astype(bf)
+
+        lane = lax.broadcasted_iota(jnp.int32, (1, 256), 1)
+
+        def attend(b):
+            def one(h, _):
+                first = h * HD
+                ks = pl.multiple_of((first // 128) * 128, 128)
+                vs = pl.multiple_of(jnp.minimum(((576 + first) // 128) * 128, 896), 128)
+                off = first - ks
+                here = (lane >= off) & (lane < off + HD)
+                q = qb[b, :, pl.ds(ks, 256)]
+                q = jnp.where(here, q, jnp.zeros_like(q))
+                s = lax.dot_general(
+                    q, kvb[b, :, pl.ds(ks, 256)], NT, preferred_element_type=f32
+                )
+                fresh, old = s[:, :256], s[:, 256:]
+                top = jnp.maximum(
+                    jnp.max(fresh, axis=1, keepdims=True), jnp.max(old, axis=1, keepdims=True) + 2.0
+                )
+                p0 = jnp.exp2(fresh - top)
+                p1 = jnp.exp2(old - (top - 2.0))
+                mass = jnp.sum(p0, axis=1, keepdims=True) + jnp.sum(p1, axis=1, keepdims=True)
+                o = jnp.dot(
+                    p0.astype(bf), kvb[b, pl.ds(0, 256), pl.ds(vs, 256)],
+                    preferred_element_type=f32,
+                ) + jnp.dot(
+                    p1.astype(bf), kvb[b, pl.ds(256, NKEY - 256), pl.ds(vs, 256)],
+                    preferred_element_type=f32,
+                )
+                o = (o * (1.0 / mass)).astype(bf)
+                voff = 576 + first - vs
+                mine = (lane >= voff) & (lane < voff + HD)
+                ws = pl.multiple_of(vs - 512, 128)
+                att[b, :, pl.ds(ws, 256)] = jnp.where(mine, o, att[b, :, pl.ds(ws, 256)])
+                return 0
+
+            lax.fori_loop(0, 8, one, 0)
+
+        def project(b):
+            rows = pl.ds(pl.multiple_of(head * 128, 128), 128)
+            p = jnp.dot(att[b, rows, :], owb[pl.ds(0, 640), :], preferred_element_type=f32)
+            p = p + jnp.dot(attr[b], owb[pl.ds(640, 640), :], preferred_element_type=f32)
+            t = tok[pl.ds(pl.multiple_of(b * 256 + head * 128, 128), 128), :].astype(f32)
+            m = (t + modrow(b, 2) * p).astype(bf)
+            mid[pl.ds(b * 128, 128), :] = m
+            n = norm(m.astype(f32)) * (1.0 + modrow(b, 4)) + modrow(b, 3)
+            n2[pl.ds(b * 128, 128), :] = n.astype(bf)
+
+        def feed(first, count):
+            def one(i, _):
+                r = pl.ds(pl.multiple_of(first + i * 768, 256), 768)
+                hid = lax.dot_general(n2[...], wb[0, r, :], NT, preferred_element_type=f32)
+                hid = jax.nn.gelu(hid, approximate=True).astype(bf)
+                acc[...] += jnp.dot(hid, wb[1, r, :], preferred_element_type=f32)
+                return 0
+
+            lax.fori_loop(0, count, one, 0)
+
+        def kstep(d, b):
+            got(f"R{d}_{b}")
+            got(f"L{d}_{b}")
+            if d < 4:
+                go(f"R{d + 1}_{b}")
+                go(f"L{d + 1}_{b}")
+
+        def fwd(tag):
+            got(tag + "1")
+            go(tag + "3a")
+            got(tag + "2")
+            go(tag + "3b")
+
+        def done(tag):
+            got(tag + "3a")
+            got(tag + "3b")
+
+        qkv(0)
+        kstep(1, 0)
+        qkv(1)
+        kstep(1, 1)
+        qkv(2)
+        kstep(1, 2)
+        kstep(2, 0)
+        fwd("A")
+        for g in (1, 2):
+            go(f"B{g}1")
+            go(f"B{g}2")
+        kstep(2, 1)
+        fwd("B0")
+        kstep(2, 2)
+        done("A")
+        go("B31")
+        go("B32")
+        got("O")
+        go("OS")
+        for b in range(3):
+            kstep(3, b)
+        done("B0")
+        go("S0")
+        for b in range(3):
+            kstep(4, b)
+            go(f"C1_{b}")
+        fwd("B1")
+        got("C0_0")
+        got("C1_0")
+        attend(0)
+        fwd("B2")
+        got("C0_1")
+        got("C1_1")
+        go("X0")
+        attend(1)
+        done("B1")
+        go("S1")
+        got("C0_2")
+        got("C1_2")
+        go("X1")
+        attend(2)
+        done("B2")
+        go("S2")
+        fwd("B3")
+        c_ow.wait()
+        got("OS")
+        got("X0")
+        project(0)
+        go("X2")
+        got("X1")
+        project(1)
+        got("X2")
+        project(2)
+        acc[...] = jnp.zeros_like(acc)
+        got("S0")
+        got("S1")
+        feed(0, 3)
+        done("B3")
+        go("S3")
+        got("S2")
+        feed(2304, 1)
+        got("S3")
+        feed(3072, 2)
+        for b in range(3):
+            r = pl.ds(b * 128, 128)
+            out_ref[r, :] = (mid[r, :].astype(f32) + modrow(b, 5) * acc[r, :]).astype(bf)
+        for c in copies.values():
+            c.wait_send()
+
+    any_spec = pl.BlockSpec(memory_space=pl.ANY)
+    n_copies = 4 + 4 * 5 + 3 * 11 + 2
+    return pl.pallas_call(
+        kernel,
+        out_shape=jax.ShapeDtypeStruct((384, D), bf),
+        in_specs=[any_spec] * 7,
+        out_specs=pl.BlockSpec(memory_space=pltpu.VMEM),
+        scratch_shapes=[
+            pltpu.VMEM((768, D), bf),
+            pltpu.VMEM((18, D), f32),
+            pltpu.VMEM((1728, D), bf),
+            pltpu.VMEM((3, NKEY, D), bf),
+            pltpu.VMEM((2, HID, D), bf),
+            pltpu.VMEM((1280, D), bf),
+            pltpu.VMEM((3, 256, 640), bf),
+            pltpu.VMEM((3, 256, 640), bf),
+            pltpu.VMEM((3, 128, 640), bf),
+            pltpu.VMEM((384, D), bf),
+            pltpu.VMEM((384, D), bf),
+            pltpu.VMEM((384, D), f32),
+            pltpu.SemaphoreType.DMA((n_copies,)),
+            pltpu.SemaphoreType.DMA((n_copies,)),
+            pltpu.SemaphoreType.DMA((6,)),
+        ],
+        compiler_params=pltpu.CompilerParams(
+            collective_id=0, has_side_effects=True, vmem_limit_bytes=64_000_000
+        ),
+    )(tok, mod, stale, wqkv, ow, fc1, fc2)
 
 
 def body(
@@ -220,87 +554,25 @@
     tokens = (jnp.einsum("bijf,fd->bijd", normed, embed_w) + pos[None]).astype(jnp.bfloat16)
     cond_part = condition(t_index, labels, t_w1, t_w2, class_table)
     cond_act = jax.nn.silu(cond_part).astype(jnp.bfloat16)
-    modulation = gathered_total(
-        jnp.dot(cond_act, ada_w, preferred_element_type=jnp.float32).astype(jnp.bfloat16), "row"
-    ).astype(jnp.float32)
-    shift1, scale1, gate1, shift2, scale2, gate2 = jnp.split(modulation, 6, axis=1)
-    per_image = tile_rows * full_cols
-    flat = tokens.astype(jnp.float32)
-    normed1 = (layer_norm(flat) * (1.0 + spread_out(scale1)) + spread_out(shift1)).astype(
-        jnp.bfloat16
-    )
+    part = jnp.dot(cond_act, ada_w, preferred_element_type=jnp.float32)
+    part = part.reshape(batch, row_count, -1).transpose(1, 0, 2)
+    piece = lax.all_to_all(part, "row", 0, 0, tiled=True).sum(axis=0)
+    modulation = copy_for_each(piece, "row").transpose(1, 0, 2).reshape(batch * 6, width)
+    half = full_cols // head_count
+    tok = tokens.reshape(batch, tile_rows, head_count, half, width).transpose(0, 2, 1, 3, 4)
+    tok = tok.reshape(batch * tile_rows * full_cols, width)
     local_width = qkv_w.shape[2]
-    heads_local = local_width // HD
-    qkv = jnp.dot(
-        normed1.reshape(batch * per_image, width),
-        qkv_w.reshape(width, 3 * local_width),
-        preferred_element_type=jnp.float32,
-    )
-    qkv = qkv.astype(jnp.bfloat16).reshape(batch, per_image, 3, heads_local, HD)
-    query = qkv[:, :, 0]
-    key_local = qkv[:, :, 1]
-    value_local = qkv[:, :, 2]
-    scale = 1.0 / math.sqrt(HD)
-    fresh = (
-        jnp.einsum("bqhd,bkhd->bhqk", query, key_local, preferred_element_type=jnp.float32) * scale
-    )
-    top_start = jnp.max(fresh, axis=-1)
-    probs = jnp.exp(fresh - top_start[..., None])
-    mass_start = jnp.sum(probs, axis=-1)
-    acc_start = jnp.einsum(
-        "bhqk,bkhd->bhqd",
-        probs.astype(jnp.bfloat16),
-        value_local,
-        preferred_element_type=jnp.float32,
-    )
-    stale_local = stale_kv.reshape(2, batch, -1, local_width)
-    per_device = stale_local.shape[2]
-    piece = lax.all_gather(stale_local, "row", axis=2, tiled=True)
-    key_count = piece.shape[2]
-    coarse_key = piece[0].reshape(batch, key_count, heads_local, HD)
-    coarse_value = piece[1].reshape(batch, key_count, heads_local, HD)
-    scores = jnp.einsum(
-        "bqhd,bkhd->bhqk", query, coarse_key, preferred_element_type=jnp.float32
-    ) * scale + math.log(4.0)
-    key_device = jnp.arange(key_count, dtype=jnp.int32) // per_device
-    scores = jnp.where((key_device == row_index)[None, None, None, :], jnp.float32(-1e30), scores)
-    new_top = jnp.maximum(top_start, jnp.max(scores, axis=-1))
-    shrink = jnp.exp(top_start - new_top)
-    weights = jnp.exp(scores - new_top[..., None])
-    new_mass = mass_start * shrink + jnp.sum(weights, axis=-1)
-    new_acc = acc_start * shrink[..., None] + jnp.einsum(
-        "bhqk,bkhd->bhqd",
-        weights.astype(jnp.bfloat16),
-        coarse_value,
-        preferred_element_type=jnp.float32,
-    )
-    attended = (new_acc / new_mass[..., None]).astype(jnp.bfloat16)
-    attended = attended.transpose(0, 2, 1, 3).reshape(batch * per_image, local_width)
-    attn_part = jnp.dot(attended, out_w, preferred_element_type=jnp.float32).reshape(
-        batch, tile_rows, full_cols, width
-    )
-    half_cols = full_cols // head_count
-    col_start = head_index * half_cols
-    projected = sent_and_summed(attn_part.astype(jnp.bfloat16), "head", 2)
-    flat_half = lax.dynamic_slice_in_dim(flat, col_start, half_cols, 2)
-    mid_half = (flat_half + spread_out(gate1) * projected).astype(jnp.bfloat16)
-    normed2_half = (
-        layer_norm(mid_half.astype(jnp.float32)) * (1.0 + spread_out(scale2)) + spread_out(shift2)
-    ).astype(jnp.bfloat16)
-    normed2 = gathered_copies(normed2_half, "head", 2)
-    normed2_rows = normed2.reshape(batch * per_image, width)
-    up_piece, down_piece = turned_gather((fc1_w, fc2_w), "col", (1, 1))
-    hidden = jax.nn.gelu(
-        jnp.dot(normed2_rows, up_piece, preferred_element_type=jnp.float32), approximate=True
-    ).astype(jnp.bfloat16)
-    mlp_part = lax.dot_general(
-        hidden, down_piece, (((1,), (1,)), ((), ())), preferred_element_type=jnp.float32
-    )
-    mlp_term = sent_and_summed(
-        mlp_part.reshape(batch, tile_rows, full_cols, width).astype(jnp.bfloat16), "head", 2
-    )
-    tokens_out = (mid_half.astype(jnp.float32) + spread_out(gate2) * mlp_term).astype(jnp.bfloat16)
-    return tokens_out
+    stale = stale_kv.transpose(1, 2, 3, 0, 4).reshape(batch, -1, 2 * local_width)
+    out = fused_block(
+        tok,
+        modulation,
+        stale,
+        qkv_w.transpose(1, 2, 0).reshape(3 * local_width, width),
+        out_w,
+        fc1_w.T,
+        fc2_w.T,
+    )
+    return out.reshape(batch, tile_rows, half, width)
 
 
 def solution(mesh):

time: 297 us -> 180 us (0.61)
  Pallas kernels: 0 us -> 110 us
  blocking collectives: 74.4 us -> 0 us
  local copies, waits for them, and re-layouts: 75.8 us -> 12.1 us
  matrix products: 53.4 us -> 1.57 us
  other arithmetic: 24.2 us -> 3.74 us
  between operations: 13.9 us -> 0.33 us
  waiting for transfers between devices: 32 us -> 22.4 us
  starting transfers between devices: 19.8 us -> 28.4 us
    pallas_call x0 -> x1, Pallas kernels: none -> 110 us  [fused_block(): pl.pallas_call(kernel, out_shape=jax.ShapeDtypeStruct((384, D), bf), in_s...]
    dot_general x8 -> x1, matrix products: 52.2 us -> 0.46 us  [body(): part = jnp.dot(cond_act, ada_w, preferred_element_type=jnp.float32)]
    slice x4 -> x0, local copies, waits for them, and re-layouts: 51.6 us -> none  [the longest x2 32.4 us: body(): coarse_key = piece[0].reshape(batch, key_count, heads_local, HD)]
    all_to_all x2 -> x0, blocking collectives: 46.6 us -> none  [the longest x1 23.7 us: copy_for_each(): lax.all_to_all(jnp.broadcast_to(shard[None], (devices, *shard.shape)), ax...]
    all_gather x1 -> x0, blocking collectives: 27.8 us -> none  [gathered_total(): pieces = lax.all_gather(shard, axis).astype(jnp.float32)]
    reduce_sum x8 -> x1, other arithmetic: 15.8 us -> 0.04 us  [body(): piece = lax.all_to_all(part, 'row', 0, 0, tiled=True).sum(axis=0)]
    all_to_all x1, waiting for transfers between devices: 22 us -> 8.73 us  [body(): piece = lax.all_to_all(part, 'row', 0, 0, tiled=True).sum(axis=0)]
    all_to_all x2 -> x3, starting transfers between devices: 11 us -> 16.9 us  [copy_for_each(): lax.all_to_all(jnp.broadcast_to(shard[None], (devices, *shard.shape)), ax...]
  transfers between devices with their start and end apart: 7 -> 6, of which waited for: 3 -> 5; matrix products, arithmetic and copies ran while one was open for 44% -> 5% of each run, Pallas kernels for 0% -> 0%
where the time goes in v1:
time: 180 us; the launch traced here: 179 us
  Pallas kernels  110 us (61%)
  starting transfers between devices  28.4 us (16%)
  waiting for transfers between devices  22.4 us (12%)
  local copies, waits for them, and re-layouts  12.1 us (7%)
  other arithmetic  3.74 us (2%)
    pallas_call x1, Pallas kernels, fused_block(): pl.pallas_call(kernel, out_shape=jax.ShapeDtypeStruct((384, D), bf), in_s...  110 us
    all_to_all x3, starting transfers between devices, copy_for_each(): lax.all_to_all(jnp.broadcast_to(shard[None], (devices, *shard.shape)), ax...  16.9 us
    all_to_all x3, waiting for transfers between devices, copy_for_each(): lax.all_to_all(jnp.broadcast_to(shard[None], (devices, *shard.shape)), ax...  10.7 us
    all_to_all x1, waiting for transfers between devices, body(): piece = lax.all_to_all(part, 'row', 0, 0, tiled=True).sum(axis=0)  8.73 us
    ppermute x1, starting transfers between devices, padded_2(): lax.ppermute(lax.slice_in_dim(block, block.shape[dim] - width, None, axis...  5.66 us
    unnamed x22, local copies, waits for them, and re-layouts  4.46 us
    all_to_all x1, starting transfers between devices, body(): piece = lax.all_to_all(part, 'row', 0, 0, tiled=True).sum(axis=0)  3.96 us
  transfers between devices with their start and end apart: 6, of which 5 were waited for; matrix products, arithmetic and copies ran while one was open for 5% of the time, Pallas kernels for 0%

profile of v1, /device:TPU:1, one launch (start us, length us, event | category | flops | bytes accessed | tf_op | source)
XLA Modules:
  0.0 178.8 jit_solution(10429944474529084458)
XLA Ops:
  0.0 0.8 broadcast_bitcast_fusion
  0.8 0.7 reshape.148
  1.5 4.8 %all-to-all-start = ((f32[2,1,1536]{2,1,0:T(1,128)}), f32[2,1,1536]{2,1,0:T(1,128)S(1)}, u32[]{:S(2)}, u32[]{:S(2)}) async-start(f32[2,1,1536]{2,1,0:T(1,128)} %reshape.148), calls=%async_computation | async-start | bytes 24576 | tf_op jit(solution)/shard_map/all_to_all | solution.py:16
  6.4 0.3 reduce-window.9
  7.0 0.4 fusion.2
  7.5 0.7 convert_element_type.24
  8.5 0.2 pad_maximum_fusion
  8.8 0.6 copy-done.1
  9.5 0.4 fusion.19
  10.0 0.5 all-to-all-done
  10.6 0.5 broadcast.125
  11.1 0.7 reduce.7
  12.0 5.7 %collective-permute-start = (f32[3,1,64,4]{2,3,1,0:T(4,128)S(1)}, f32[3,1,64,4]{2,3,1,0:T(4,128)S(1)}, u32[]{:S(2)}, u32[]{:S(2)}) collective-permute-start(f32[3,1,64,4]{2,3,1,0:T(4,128)S(1)} %get-tuple-element.18), channel_id=1, source_target_pairs={{0,16},{16,32},{32,48},{48,64},{64,80},{80,96},{96,112},{112,128},... | collective-permute-start | bytes 9224 | tf_op jit(solution)/shard_map/ppermute | solution.py:37
  17.7 1.9 %collective-permute-start.1 = (f32[3,1,64,4]{2,3,1,0:T(4,128)S(1)}, f32[3,1,64,4]{2,3,1,0:T(4,128)S(1)}, u32[]{:S(2)}, u32[]{:S(2)}) collective-permute-start(f32[3,1,64,4]{2,3,1,0:T(4,128)S(1)} %get-tuple-element.19), channel_id=1, source_target_pairs={{16,0},{32,16},{48,32},{64,48},{80,64},{96,80},{112,96},{128,112},... | collective-permute-start | bytes 9224 | tf_op jit(solution)/shard_map/ppermute | solution.py:40
  19.7 3.0 %collective-permute-done.1 = f32[3,1,64,4]{2,3,1,0:T(4,128)S(1)} collective-permute-done((f32[3,1,64,4]{2,3,1,0:T(4,128)S(1)}, f32[3,1,64,4]{2,3,1,0:T(4,128)S(1)}, u32[]{:S(2)}, u32[]{:S(2)}) %collective-permute-start.1) | collective-permute-done | bytes 3104 | tf_op jit(solution)/shard_map/ppermute | solution.py:40
  23.8 0.6 broadcast_in_dim.11
  24.4 8.4 %all-to-all-start.1 = ((f32[16,1,24]{2,1,0:T(1,128)}), f32[16,1,24]{2,1,0:T(1,128)S(1)}, u32[]{:S(2)}, u32[]{:S(2)}) async-start(f32[16,1,24]{2,1,0:T(1,128)} %broadcast_in_dim.11), calls=%async_computation.1 | async-start | bytes 16384 | tf_op jit(solution)/shard_map/all_to_all | solution.py:16
  32.9 0.5 fusion.36
  33.5 0.7 copy.55
  34.2 0.5 copy.52
  34.7 1.1 reshape.143.stale_h
  35.8 4.1 %all-to-all-done.1 = f32[16,1,24]{2,1,0:T(1,128)S(1)} async-done(((f32[16,1,24]{2,1,0:T(1,128)}), f32[16,1,24]{2,1,0:T(1,128)S(1)}, u32[]{:S(2)}, u32[]{:S(2)}) %all-to-all-start.1) | async-done | bytes 1568 | tf_op jit(solution)/shard_map/all_to_all | solution.py:16
  39.9 4.0 %all-to-all-start.2 = ((f32[16,3,432]{2,1,0:T(4,128)}), f32[16,3,432]{2,1,0:T(4,128)S(1)}, u32[]{:S(2)}, u32[]{:S(2)}) async-start(f32[16,3,432]{2,1,0:T(4,128)} %bitcast.58), calls=%async_computation.2 | async-start | bytes 262144 | tf_op jit(solution)/shard_map/all_to_all | solution.py:559
  44.3 8.7 %all-to-all-done.2 = f32[16,3,432]{2,1,0:T(4,128)S(1)} async-done(((f32[16,3,432]{2,1,0:T(4,128)}), f32[16,3,432]{2,1,0:T(4,128)S(1)}, u32[]{:S(2)}, u32[]{:S(2)}) %all-to-all-start.2) | async-done | bytes 82976 | tf_op jit(solution)/shard_map/all_to_all | solution.py:559
  53.1 0.7 broadcast_in_dim.14
  53.8 3.6 %all-to-all-start.3 = ((f32[16,3,432]{2,1,0:T(4,128)}), f32[16,3,432]{2,1,0:T(4,128)S(1)}, u32[]{:S(2)}, u32[]{:S(2)}) async-start(f32[16,3,432]{2,1,0:T(4,128)} %broadcast_in_dim.14), calls=%async_computation.3 | async-start | bytes 262144 | tf_op jit(solution)/shard_map/all_to_all | solution.py:16
  57.4 0.7 fusion
  58.1 1.4 copy.49
  59.5 6.1 %all-to-all-done.3 = f32[16,3,432]{2,1,0:T(4,128)S(1)} async-done(((f32[16,3,432]{2,1,0:T(4,128)}), f32[16,3,432]{2,1,0:T(4,128)S(1)}, u32[]{:S(2)}, u32[]{:S(2)}) %all-to-all-start.3) | async-done | bytes 82976 | tf_op jit(solution)/shard_map/all_to_all | solution.py:16
  65.7 0.8 reshape.142.mod_h
  66.5 110.2 %shard_map.136 = bf16[384,1152]{1,0:T(8,128)(2,1)} custom-call(bf16[768,1152]{1,0:T(8,128)(2,1)} %bitcast.61, f32[18,1152]{1,0:T(8,128)} %reshape.142.mod_h, bf16[3,64,1152]{2,1,0:T(8,128)(2,1)} %reshape.143.stale_h, bf16[1728,1152]{1,0:T(8,128)(2,1)} %bitcast.62, bf16[576,1152]{1,0:T(8,128)(2,1)} %ow_h.1, bf16[288,1152]{1,0:T(8,128)(2,1)} %bitcast.64, ...), custom_call_target="tpu_custom_call" | custom-call | tf_op jit(solution)/shard_map/pallas_call | solution.py:477
  176.7 2.2 %copy.57 = bf16[3,4,32,1152]{3,2,1,0:T(8,128)(2,1)} copy(bf16[3,4,32,1152]{3,2,1,0:T(8,128)(2,1)} %bitcast.63) | data formatting | bytes 1769472
  (70 shorter events, 3.1 us)
Async XLA Ops:
  0.0 32.8 %copy-start = (bf16[72,6912]{1,0:T(8,128)(2,1)S(1)}, bf16[72,6912]{1,0:T(8,128)(2,1)}, u32[]{:S(2)}) copy-start(bf16[72,6912]{1,0:T(8,128)(2,1)} %param.23) | copy-start | bytes 2985988
  1.5 9.0 %all-to-all-start = ((f32[2,1,1536]{2,1,0:T(1,128)}), f32[2,1,1536]{2,1,0:T(1,128)S(1)}, u32[]{:S(2)}, u32[]{:S(2)}) async-start(f32[2,1,1536]{2,1,0:T(1,128)} %reshape.148), calls=%async_computation | async-start | bytes 24576 | tf_op jit(solution)/shard_map/all_to_all | solution.py:16
  8.4 1.1 copy-start.1
  8.4 1.1 copy-start.3
  8.4 1.4 copy-start.8
  8.7 14.4 %copy-start.5 = (f32[3,4,64,16]{2,3,1,0:T(8,128)S(1)}, f32[3,4,64,16]{2,3,1,0:T(8,128)}, u32[]{:S(2)}) copy-start(f32[3,4,64,16]{2,3,1,0:T(8,128)} %param.15) | copy-start | bytes 147460
  8.7 24.1 %copy-start.4 = (bf16[1001,72]{0,1:T(8,128)(2,1)S(1)}, bf16[1001,72]{0,1:T(8,128)(2,1)}, u32[]{:S(2)}) copy-start(bf16[1001,72]{0,1:T(8,128)(2,1)} %param.22) | copy-start | bytes 432436
  8.7 24.1 %copy-start.7 = (s32[3]{0:T(128)S(1)}, s32[3]{0:T(128)}, u32[]{:S(2)}) copy-start(s32[3]{0:T(128)} %param.17) | copy-start | bytes 40
  11.9 22.3 %copy-start.2 = (bf16[2,3,2,32,576]{4,3,2,1,0:T(8,128)(2,1)S(1)}, bf16[2,3,2,32,576]{4,3,2,1,0:T(8,128)(2,1)}, u32[]{:S(2)}) copy-start(bf16[2,3,2,32,576]{4,3,2,1,0:T(8,128)(2,1)} %param.18) | copy-start | bytes 1327108
  12.0 7.6 %collective-permute-start = (f32[3,1,64,4]{2,3,1,0:T(4,128)S(1)}, f32[3,1,64,4]{2,3,1,0:T(4,128)S(1)}, u32[]{:S(2)}, u32[]{:S(2)}) collective-permute-start(f32[3,1,64,4]{2,3,1,0:T(4,128)S(1)} %get-tuple-element.18), channel_id=1, source_target_pairs={{0,16},{16,32},{32,48},{48,64},{64,80},{80,96},{96,112},{112,128},... | collective-permute-start | bytes 9224 | tf_op jit(solution)/shard_map/ppermute | solution.py:37
  17.7 4.9 %collective-permute-start.1 = (f32[3,1,64,4]{2,3,1,0:T(4,128)S(1)}, f32[3,1,64,4]{2,3,1,0:T(4,128)S(1)}, u32[]{:S(2)}, u32[]{:S(2)}) collective-permute-start(f32[3,1,64,4]{2,3,1,0:T(4,128)S(1)} %get-tuple-element.19), channel_id=1, source_target_pairs={{16,0},{32,16},{48,32},{64,48},{80,64},{96,80},{112,96},{128,112},... | collective-permute-start | bytes 9224 | tf_op jit(solution)/shard_map/ppermute | solution.py:40
  24.4 15.5 %all-to-all-start.1 = ((f32[16,1,24]{2,1,0:T(1,128)}), f32[16,1,24]{2,1,0:T(1,128)S(1)}, u32[]{:S(2)}, u32[]{:S(2)}) async-start(f32[16,1,24]{2,1,0:T(1,128)} %broadcast_in_dim.11), calls=%async_computation.1 | async-start | bytes 16384 | tf_op jit(solution)/shard_map/all_to_all | solution.py:16
  33.3 24.0 %copy-start.6 = (f32[16,1152]{1,0:T(8,128)S(1)}, f32[16,1152]{1,0:T(8,128)}, u32[]{:S(2)}) copy-start(f32[16,1152]{1,0:T(8,128)} %param.19) | copy-start | bytes 221188
  39.9 13.1 %all-to-all-start.2 = ((f32[16,3,432]{2,1,0:T(4,128)}), f32[16,3,432]{2,1,0:T(4,128)S(1)}, u32[]{:S(2)}, u32[]{:S(2)}) async-start(f32[16,3,432]{2,1,0:T(4,128)} %bitcast.58), calls=%async_computation.2 | async-start | bytes 262144 | tf_op jit(solution)/shard_map/all_to_all | solution.py:559
  53.8 11.9 %all-to-all-start.3 = ((f32[16,3,432]{2,1,0:T(4,128)}), f32[16,3,432]{2,1,0:T(4,128)S(1)}, u32[]{:S(2)}, u32[]{:S(2)}) async-start(f32[16,3,432]{2,1,0:T(4,128)} %broadcast_in_dim.14), calls=%async_computation.3 | async-start | bytes 262144 | tf_op jit(solution)/shard_map/all_to_all | solution.py:16

commit v2 on v1

--- a/solution.py
+++ b/solution.py
@@ -170,18 +170,19 @@
     return vector[:, None, None, :]
 
 
-def fused_block(tok, mod, stale, wqkv, ow, fc1, fc2):
+def fused_block(levels, x_lo, noise, embed, pos, part, stale, wqkv, ow, fc1, fc2):
     D = 1152
     L2E = 1.4426950408889634
     QS = L2E / math.sqrt(HD)
     bf, f32 = jnp.bfloat16, jnp.float32
     NKEY = 256 + 15 * 64
     HID = 4608
-    names = []
+    UNROLL = 2
 
     def kernel(
-        tok_h, mod_h, stale_h, wqkv_h, ow_h, fc1_h, fc2_h, out_ref,
-        tok, mod, wq, kvb, wb, owb, qb, att, attr, n2, mid, acc, send, recv, local,
+        levels_s, x_h, noise_h, embed_h, pos_h, part_h, stale_h, wqkv_h, ow_h, fc1_h, fc2_h, out_ref,
+        xn, nz, emb, pos, part, rsb, redc, modp, st, stb, noisy,
+        tok, wq, kvb, wb, owb, qb, att, attr, n2, mid, acc, send, recv, local,
     ):
         row, col, head = lax.axis_index("row"), lax.axis_index("col"), lax.axis_index("head")
         z, core = row // 2, row % 2
@@ -201,6 +202,11 @@
             "far": at((x + 2) % 4, y, z, core),
         }
         other = at(3 - x, y, z, core)
+        twin = at(x, y, z + 1 - 2 * (z % 2), core)
+        near = {}
+        for dr in (1, 15):
+            near[f"h{dr}"] = ((row + dr) % 16, col, 1 - head)
+        fellows = {k: ((row + k) % 16, col, head) for k in range(1, 16)}
 
         copies = {}
         order = {"n": 0}
@@ -273,27 +279,56 @@
                 peers["sib"],
             )
             remote(
-                f"X{b}", att.at[b, pl.ds(pl.multiple_of((1 - head) * 128, 128), 128), :],
-                attr.at[b], peers["far"],
+                f"X{b}", att.at[b, :, 1 - head], attr.at[b], peers["far"],
             )
-        ow_own = pl.ds(pl.multiple_of(core * 288, 16), 288)
-        ow_far = pl.ds(pl.multiple_of(704 + core * 288, 16), 288)
-        remote("O", ow_h.at[ow_own, :], owb.at[ow_far, :], other)
-        remote("OS", owb.at[ow_far, :], owb.at[ow_far, :], peers["sib"])
+        part_at = lambda p: p * 288 + core * 144
+        ow_own = pl.ds(pl.multiple_of(part_at(z % 2), 16), 144)
+        far0 = pl.ds(pl.multiple_of(704 + part_at(z % 2), 16), 144)
+        far1 = pl.ds(pl.multiple_of(704 + part_at(1 - z % 2), 16), 144)
+        remote("O", ow_h.at[ow_own, :], owb.at[far0, :], other)
+        remote("OZ", owb.at[far0, :], owb.at[far0, :], twin)
+        remote("OS0", owb.at[far0, :], owb.at[far0, :], peers["sib"])
+        remote("OS1", owb.at[far1, :], owb.at[far1, :], peers["sib"])
+        remote("Pf", xn.at[1, head], xn.at[1, head], peers["far"])
+        remote("Pd", xn.at[1, head], xn.at[0, head], fellows[1])
+        remote("Pu", xn.at[1, head], xn.at[2, head], fellows[15])
+        remote("Pdf", xn.at[1, head], xn.at[0, head], near["h1"])
+        remote("Puf", xn.at[1, head], xn.at[2, head], near["h15"])
+        for k in range(1, 16):
+            to = (row + k) % 16
+            chunk = pl.ds(pl.multiple_of(to * 256, 256), 256)
+            mine = pl.ds(pl.multiple_of(row * 256, 256), 256)
+            remote(f"M{k}", part.at[:, chunk], rsb.at[k], fellows[k])
+            remote(f"G{k}", redc, modp.at[:, mine], fellows[k])
+            remote(f"T{k}", st, stb.at[k], fellows[k])
 
         c_w1 = load(fc1_h.at[half_own, :], wb.at[0, pl.ds(0, 144), :])
         c_w2 = load(fc2_h.at[half_own, :], wb.at[1, pl.ds(0, 144), :])
-        c_tok = load(tok_h, tok)
-        c_mod = load(mod_h, mod)
+        c_x = load(x_h, xn.at[1, head])
+        c_part = load(part_h, part)
+        c_nz = load(noise_h, nz)
+        c_emb = load(embed_h, emb)
+        c_pos = load(pos_h, pos)
         c_wq = load(wqkv_h, wq)
         c_ow = load(ow_h, owb.at[pl.ds(64, 576), :])
         barrier = pltpu.get_barrier_semaphore()
-        for peer in peers.values():
+        greet = list(fellows.values()) + list(near.values())
+        greet += [peers[n] for n in ("ap", "am", "bp", "bm", "far")]
+        for peer in greet:
             pl.semaphore_signal(barrier, inc=1, device_id=peer, device_id_type=pl.DeviceIdType.MESH)
-        pl.semaphore_wait(barrier, len(peers))
-        for b in range(3):
-            go(f"R1_{b}")
-            go(f"L1_{b}")
+        owb[pl.ds(0, 64), :] = jnp.zeros((64, D), bf)
+        owb[pl.ds(640, 64), :] = jnp.zeros((64, D), bf)
+        att[...] = jnp.zeros_like(att)
+        acc[...] = jnp.zeros_like(acc)
+        c_x.wait()
+        c_part.wait()
+        pl.semaphore_wait(barrier, len(greet))
+        for n in ("Pf", "Pd", "Pu", "Pdf", "Puf"):
+            go(n)
+        for k in range(1, 16):
+            go(f"M{k}")
+        go("R1_0")
+        go("L1_0")
         c_w1.wait()
         c_w2.wait()
         for n in ("A1", "A2", "B01", "B02"):
@@ -301,13 +336,66 @@
         for b in range(3):
             go(f"C0_{b}")
         go("O")
-
-        owb[pl.ds(0, 64), :] = jnp.zeros((64, D), bf)
-        owb[pl.ds(640, 64), :] = jnp.zeros((64, D), bf)
-        att[...] = jnp.zeros_like(att)
-        c_tok.wait()
-        c_mod.wait()
-        c_wq.wait()
+        c_nz.wait()
+        c_emb.wait()
+        for n in ("Pf", "Pd", "Pu", "Pdf", "Puf"):
+            got(n)
+
+        def line(d, i):
+            return jnp.concatenate([xn[d, 0, :, i], xn[d, 1, :, i]], axis=-1)
+
+        lines = [line(0, 3)] + [line(1, i) for i in range(4)] + [line(2, 0)]
+        lines[0] = jnp.where(row == 0, lines[1], lines[0])
+        lines[5] = jnp.where(row == 15, lines[4], lines[5])
+        image = lax.broadcasted_iota(jnp.int32, (3, 4, 64), 0)
+
+        def per_image(k):
+            return jnp.where(
+                image == 0, levels_s[k], jnp.where(image == 1, levels_s[k + 1], levels_s[k + 2])
+            )
+
+        keep, fuzz = per_image(0), per_image(3)
+        total = jnp.zeros((3, 4, 64), f32)
+        square = jnp.zeros((3, 4, 64), f32)
+        for i in range(4):
+            for di in range(2):
+                v = 0.75 * lines[i + 1] + 0.25 * lines[i + 2 * di]
+                sides = (
+                    jnp.concatenate([v[:, :, :1], v[:, :, :63]], axis=-1),
+                    jnp.concatenate([v[:, :, 1:], v[:, :, 63:]], axis=-1),
+                )
+                for dj in range(2):
+                    k = 2 * di + dj
+                    n = keep * (0.75 * v + 0.25 * sides[dj]) + fuzz * nz[:, i, 4 * k : 4 * k + 4, :]
+                    noisy[:, i, 4 * k : 4 * k + 4, :] = n
+                    total = total + n
+                    square = square + n * n
+        lane1 = lax.broadcasted_iota(jnp.int32, (8, 128), 1)
+        both = jnp.zeros((8, 128), f32)
+        for b in range(3):
+            s = jnp.concatenate(
+                [
+                    jnp.sum(total[b], axis=1, keepdims=True),
+                    jnp.sum(square[b], axis=1, keepdims=True),
+                ],
+                axis=0,
+            )
+            both = jnp.where(lane1 == b, jnp.broadcast_to(s, (8, 128)), both)
+        st[...] = both
+        for k in range(1, 16):
+            got(f"M{k}")
+        mine = pl.ds(pl.multiple_of(row * 256, 256), 256)
+        piece = part[:, mine]
+        for k in range(1, 16):
+            piece = piece + rsb[k]
+        redc[...] = piece
+        modp[:, mine] = piece
+        for k in range(1, 16):
+            go(f"T{k}")
+        for k in range(1, 16):
+            go(f"G{k}")
+        go("R1_1")
+        go("L1_1")
 
         def norm(v):
             centre = jnp.mean(v, axis=-1, keepdims=True)
@@ -316,13 +404,13 @@
             return v * lax.rsqrt(spread + 1e-06)
 
         def modrow(b, k):
-            return mod[pl.ds(b * 6 + k, 1), :]
+            return modp[pl.ds(b + 4 * (k // 3), 1), pl.ds((k % 3) * D, D)]
 
         NT = (((1,), (1,)), ((), ()))
 
         def qkv(b):
             n1 = (
-                norm(tok[pl.ds(b * 256, 256), :].astype(f32)) * (1.0 + modrow(b, 1)) + modrow(b, 0)
+                norm(tok[b].reshape(256, D).astype(f32)) * (1.0 + modrow(b, 1)) + modrow(b, 0)
             ).astype(bf)
             q = lax.dot_general(n1, wq[pl.ds(0, 576), :], NT, preferred_element_type=f32)
             qb[b, :, pl.ds(0, 576)] = (q * QS).astype(bf)
@@ -332,17 +420,20 @@
         lane = lax.broadcasted_iota(jnp.int32, (1, 256), 1)
 
         def attend(b):
-            def one(h, _):
+            def score(h):
                 first = h * HD
                 ks = pl.multiple_of((first // 128) * 128, 128)
-                vs = pl.multiple_of(jnp.minimum(((576 + first) // 128) * 128, 896), 128)
                 off = first - ks
                 here = (lane >= off) & (lane < off + HD)
                 q = qb[b, :, pl.ds(ks, 256)]
                 q = jnp.where(here, q, jnp.zeros_like(q))
-                s = lax.dot_general(
+                return lax.dot_general(
                     q, kvb[b, :, pl.ds(ks, 256)], NT, preferred_element_type=f32
                 )
+
+            def mix(h, s):
+                first = h * HD
+                vs = pl.multiple_of(jnp.minimum(((576 + first) // 128) * 128, 896), 128)
                 fresh, old = s[:, :256], s[:, 256:]
                 top = jnp.maximum(
                     jnp.max(fresh, axis=1, keepdims=True), jnp.max(old, axis=1, keepdims=True) + 2.0
@@ -357,20 +448,28 @@
                     p1.astype(bf), kvb[b, pl.ds(256, NKEY - 256), pl.ds(vs, 256)],
                     preferred_element_type=f32,
                 )
-                o = (o * (1.0 / mass)).astype(bf)
+                o = (o * (1.0 / mass)).astype(bf).reshape(4, 2, 32, 256)
                 voff = 576 + first - vs
                 mine = (lane >= voff) & (lane < voff + HD)
                 ws = pl.multiple_of(vs - 512, 128)
-                att[b, :, pl.ds(ws, 256)] = jnp.where(mine, o, att[b, :, pl.ds(ws, 256)])
+                att[b, :, :, :, pl.ds(ws, 256)] = jnp.where(
+                    mine.reshape(1, 1, 1, 256), o, att[b, :, :, :, pl.ds(ws, 256)]
+                )
+
+            def some(i, _):
+                hs = [i * UNROLL + j for j in range(UNROLL)]
+                ss = [score(h) for h in hs]
+                for h, s in zip(hs, ss):
+                    mix(h, s)
                 return 0
 
-            lax.fori_loop(0, 8, one, 0)
+            lax.fori_loop(0, 8 // UNROLL, some, 0)
 
         def project(b):
-            rows = pl.ds(pl.multiple_of(head * 128, 128), 128)
-            p = jnp.dot(att[b, rows, :], owb[pl.ds(0, 640), :], preferred_element_type=f32)
-            p = p + jnp.dot(attr[b], owb[pl.ds(640, 640), :], preferred_element_type=f32)
-            t = tok[pl.ds(pl.multiple_of(b * 256 + head * 128, 128), 128), :].astype(f32)
+            mine = att[b, :, head].reshape(128, 640)
+            p = jnp.dot(mine, owb[pl.ds(0, 640), :], preferred_element_type=f32)
+            p = p + jnp.dot(attr[b].reshape(128, 640), owb[pl.ds(640, 640), :], preferred_element_type=f32)
+            t = tok[b, :, head].reshape(128, D).astype(f32)
             m = (t + modrow(b, 2) * p).astype(bf)
             mid[pl.ds(b * 128, 128), :] = m
             n = norm(m.astype(f32)) * (1.0 + modrow(b, 4)) + modrow(b, 3)
@@ -403,60 +502,99 @@
             got(tag + "3a")
             got(tag + "3b")
 
+        kstep(1, 0)
+        for k in range(1, 16):
+            got(f"T{k}")
+        both = st[...]
+        for k in range(1, 16):
+            both = both + stb[k]
+        shares, gains = [], []
+        for b in range(3):
+            col_b = jnp.sum(jnp.where(lane1 == b, both, 0.0), axis=1, keepdims=True) / 16384.0
+            centre = col_b[0:4]
+            gain = lax.rsqrt(col_b[4:8] - centre * centre + 1e-05)
+            shares.append(jnp.concatenate([centre] * 4, axis=0))
+            gains.append(jnp.concatenate([gain] * 4, axis=0))
+        whi = emb[...].astype(bf)
+        wlo = (emb[...] - whi.astype(f32)).astype(bf)
+        w3 = jnp.concatenate([whi, whi, wlo], axis=0)
+        c_pos.wait()
+        c_wq.wait()
+        for b in range(3):
+            for i in range(4):
+                n = (noisy[b, i] - shares[b]) * gains[b]
+                hi = n.astype(bf)
+                lo = (n - hi.astype(f32)).astype(bf)
+                e = lax.dot_general(
+                    jnp.concatenate([hi, lo, hi], axis=0), w3, (((0,), (0,)), ((), ())),
+                    preferred_element_type=f32,
+                )
+                e = (e + pos[pl.ds(i * 64, 64), :]).astype(bf)
+                tok[b, i] = e.reshape(2, 32, D)
+        for k in range(1, 16):
+            got(f"G{k}")
+        kstep(1, 1)
         qkv(0)
-        kstep(1, 0)
-        qkv(1)
-        kstep(1, 1)
-        qkv(2)
-        kstep(1, 2)
         kstep(2, 0)
         fwd("A")
+        fwd("B0")
         for g in (1, 2):
             go(f"B{g}1")
             go(f"B{g}2")
+        qkv(1)
         kstep(2, 1)
-        fwd("B0")
-        kstep(2, 2)
+        qkv(2)
+        got("O")
+        go("OZ")
+        go("OS0")
+        kstep(3, 0)
         done("A")
         go("B31")
         go("B32")
-        got("O")
-        go("OS")
-        for b in range(3):
-            kstep(3, b)
-        done("B0")
-        go("S0")
-        for b in range(3):
-            kstep(4, b)
-            go(f"C1_{b}")
-        fwd("B1")
+        kstep(3, 1)
+        kstep(4, 0)
+        go("C1_0")
+        go("R1_2")
+        go("L1_2")
+        got("OZ")
+        go("OS1")
         got("C0_0")
         got("C1_0")
         attend(0)
-        fwd("B2")
+        kstep(4, 1)
+        go("C1_1")
+        kstep(1, 2)
+        done("B0")
+        go("S0")
+        fwd("B1")
+        go("X0")
         got("C0_1")
         got("C1_1")
-        go("X0")
+        kstep(2, 2)
         attend(1)
+        kstep(3, 2)
+        fwd("B2")
+        go("X1")
+        c_ow.wait()
+        got("OS0")
+        got("OS1")
+        got("X0")
+        project(0)
+        kstep(4, 2)
+        go("C1_2")
+        fwd("B3")
         done("B1")
         go("S1")
         got("C0_2")
         got("C1_2")
-        go("X1")
         attend(2)
-        done("B2")
-        go("S2")
-        fwd("B3")
-        c_ow.wait()
-        got("OS")
-        got("X0")
-        project(0)
         go("X2")
         got("X1")
         project(1)
+        done("B2")
+        go("S2")
         got("X2")
         project(2)
-        acc[...] = jnp.zeros_like(acc)
         got("S0")
         got("S1")
         feed(0, 3)
@@ -473,33 +611,43 @@
             c.wait_send()
 
     any_spec = pl.BlockSpec(memory_space=pl.ANY)
-    n_copies = 4 + 4 * 5 + 3 * 11 + 2
+    n_copies = 4 + 4 * 5 + 3 * 11 + 4 + 5 + 45
     return pl.pallas_call(
         kernel,
         out_shape=jax.ShapeDtypeStruct((384, D), bf),
-        in_specs=[any_spec] * 7,
+        in_specs=[pl.BlockSpec(memory_space=pltpu.SMEM)] + [any_spec] * 10,
         out_specs=pl.BlockSpec(memory_space=pltpu.VMEM),
         scratch_shapes=[
-            pltpu.VMEM((768, D), bf),
-            pltpu.VMEM((18, D), f32),
+            pltpu.VMEM((3, 2, 3, 4, 4, 32), f32),
+            pltpu.VMEM((3, 4, 16, 64), f32),
+            pltpu.VMEM((16, D), f32),
+            pltpu.VMEM((256, D), f32),
+            pltpu.VMEM((8, 4096), f32),
+            pltpu.VMEM((16, 8, 256), f32),
+            pltpu.VMEM((8, 256), f32),
+            pltpu.VMEM((8, 4096), f32),
+            pltpu.VMEM((8, 128), f32),
+            pltpu.VMEM((16, 8, 128), f32),
+            pltpu.VMEM((3, 4, 16, 64), f32),
+            pltpu.VMEM((3, 4, 2, 32, D), bf),
             pltpu.VMEM((1728, D), bf),
             pltpu.VMEM((3, NKEY, D), bf),
             pltpu.VMEM((2, HID, D), bf),
             pltpu.VMEM((1280, D), bf),
             pltpu.VMEM((3, 256, 640), bf),
-            pltpu.VMEM((3, 256, 640), bf),
-            pltpu.VMEM((3, 128, 640), bf),
+            pltpu.VMEM((3, 4, 2, 32, 640), bf),
+            pltpu.VMEM((3, 4, 32, 640), bf),
             pltpu.VMEM((384, D), bf),
             pltpu.VMEM((384, D), bf),
             pltpu.VMEM((384, D), f32),
             pltpu.SemaphoreType.DMA((n_copies,)),
             pltpu.SemaphoreType.DMA((n_copies,)),
-            pltpu.SemaphoreType.DMA((6,)),
+            pltpu.SemaphoreType.DMA((9,)),
         ],
         compiler_params=pltpu.CompilerParams(
             collective_id=0, has_side_effects=True, vmem_limit_bytes=64_000_000
         ),
-    )(tok, mod, stale, wqkv, ow, fc1, fc2)
+    )(levels, x_lo, noise, embed, pos, part, stale, wqkv, ow, fc1, fc2)
 
 
 def body(
@@ -528,44 +676,24 @@
     channels = x_lo.shape[3]
     width = embed_w.shape[1]
     abar = noise_level(t_index)
-    gathered = gathered_copies(x_lo, "head", 2)
-    padded = padded_2(gathered, (("row", 1),), 1)
-    padded = clamp_edges(padded, 1, row_index == 0, row_index == row_count - 1)
-    padded = jnp.pad(padded, ((0, 0), (0, 0), (1, 1), (0, 0)), mode="edge")
-    upsampled = upsample_padded(padded)
-    noisy = (
-        jnp.sqrt(abar)[:, None, None, None] * upsampled
-        + jnp.sqrt(1.0 - abar)[:, None, None, None] * noise
-    )
-    grouped = noisy.reshape(batch, tile_rows, full_cols, 4, channels)
-    total, squares = together(
-        (jnp.sum(grouped, axis=(1, 2, 3)), jnp.sum(grouped * grouped, axis=(1, 2, 3))), "row"
-    )
-    count = 4.0 * tile_rows * row_count * full_cols
-    centre = total / count
-    spread = squares / count - centre * centre
-    normed = (
-        (grouped - centre[:, None, None, None, :])
-        * lax.rsqrt(spread + 1e-05)[:, None, None, None, :]
-    ).reshape(batch, tile_rows, full_cols, 4 * channels)
     row_pos = (row_index * tile_rows + jnp.arange(tile_rows, dtype=jnp.int32)).astype(jnp.float32)
     col_pos = jnp.arange(full_cols, dtype=jnp.float32)
     pos = position_table(row_pos, col_pos, width)
-    tokens = (jnp.einsum("bijf,fd->bijd", normed, embed_w) + pos[None]).astype(jnp.bfloat16)
     cond_part = condition(t_index, labels, t_w1, t_w2, class_table)
     cond_act = jax.nn.silu(cond_part).astype(jnp.bfloat16)
     part = jnp.dot(cond_act, ada_w, preferred_element_type=jnp.float32)
-    part = part.reshape(batch, row_count, -1).transpose(1, 0, 2)
-    piece = lax.all_to_all(part, "row", 0, 0, tiled=True).sum(axis=0)
-    modulation = copy_for_each(piece, "row").transpose(1, 0, 2).reshape(batch * 6, width)
+    part = part.reshape(batch, 2, 3 * width).transpose(1, 0, 2)
+    part = jnp.pad(part, ((0, 0), (0, 1), (0, 4096 - 3 * width))).reshape(8, 4096)
     half = full_cols // head_count
-    tok = tokens.reshape(batch, tile_rows, head_count, half, width).transpose(0, 2, 1, 3, 4)
-    tok = tok.reshape(batch * tile_rows * full_cols, width)
     local_width = qkv_w.shape[2]
     stale = stale_kv.transpose(1, 2, 3, 0, 4).reshape(batch, -1, 2 * local_width)
     out = fused_block(
-        tok,
-        modulation,
+        jnp.concatenate([jnp.sqrt(abar), jnp.sqrt(1.0 - abar)]),
+        x_lo.transpose(0, 1, 3, 2),
+        noise.transpose(0, 1, 3, 2),
+        embed_w,
+        pos.reshape(-1, width),
+        part,
         stale,
         qkv_w.transpose(1, 2, 0).reshape(3 * local_width, width),
         out_w,

time: 180 us -> 114 us (0.63)
  starting transfers between devices: 28.4 us -> 0 us
  waiting for transfers between devices: 22.4 us -> 0 us
  local copies, waits for them, and re-layouts: 12.1 us -> 4.84 us
  Pallas kernels: 110 us -> 105 us
    all_to_all x4 -> x0, starting transfers between devices: 20.8 us -> none  [the longest x3 16.9 us: copy_for_each(): lax.all_to_all(jnp.broadcast_to(shard[None], (devices, *shard.shape)), ax...]
    all_to_all x4 -> x0, waiting for transfers between devices: 19.5 us -> none  [the longest x3 10.7 us: copy_for_each(): lax.all_to_all(jnp.broadcast_to(shard[None], (devices, *shard.shape)), ax...]
    ppermute x2 -> x0, starting transfers between devices: 7.59 us -> none  [the longest x1 5.66 us: padded_2(): lax.ppermute(lax.slice_in_dim(block, block.shape[dim] - width, None, axis...]
    pallas_call x1, Pallas kernels: 110 us -> 105 us  [fused_block(): pl.pallas_call(kernel, out_shape=jax.ShapeDtypeStruct((384, D), bf), in_s...]
    ppermute x2 -> x0, waiting for transfers between devices: 2.99 us -> none  [the longest x1 2.99 us: padded_2(): lax.ppermute(lax.slice_in_dim(block, 0, width, axis=dim), axis, backward)]
    reshape x8 -> x2, local copies, waits for them, and re-layouts: 3.3 us -> 0.7 us  [the longest x1 0.7 us: body(): jnp.pad(part, ((0, 0), (0, 1), (0, 4096 - 3 * width))).reshape(8, 4096)]
    unnamed x22 -> x15, local copies, waits for them, and re-layouts: 4.46 us -> 2.21 us
  transfers between devices with their start and end apart: 6 -> 0, of which waited for: 5 -> 0; matrix products, arithmetic and copies ran while one was open for 5% -> 0% of each run, Pallas kernels for 0% -> 0%
where the time goes in v2:
time: 114 us
  Pallas kernels  105 us (92%)
  local copies, waits for them, and re-layouts  4.84 us (4%)
  other arithmetic  3.23 us (3%)
    pallas_call x1, Pallas kernels, fused_block(): pl.pallas_call(kernel, out_shape=jax.ShapeDtypeStruct((384, D), bf), in_s...  105 us

profile of v2, /device:TPU:1, one launch (start us, length us, event | category | flops | bytes accessed | tf_op | source)
XLA Modules:
  0.0 113.6 jit_solution(13828025485661608551)
XLA Ops:
  0.0 0.0 copy-start
  0.0 0.4 fusion.1
  0.4 0.1 pad_maximum_fusion.1
  0.5 0.1 multiply_sine_fusion
  0.7 0.1 pad_maximum_fusion.2
  0.8 0.0 copy-start.6
  0.8 0.0 copy-start.1
  0.8 0.0 copy-start.3
  0.8 0.0 copy-start.4
  0.9 0.0 copy-start.5
  0.9 1.2 %pad_maximum_fusion = f32[4,64,1152]{2,1,0:T(8,128)} fusion(f32[4,64,576]{2,1,0:T(8,128)S(1)} %broadcast_in_dim.5, f32[4,64,576]{2,1,0:T(8,128)S(1)} %broadcast_in_dim.4), kind=kLoop, calls=%fused_computation | loop fusion | flops 294912 | bytes 2359296 | tf_op jit(solution)/shard_map/concatenate | solution.py:139
  2.1 0.3 reduce-window.9
  2.4 0.1 slice.10
  2.5 0.1 slice_reduce_fusion
  2.6 0.1 add_bitcast_fusion
  2.7 0.0 copy-done.6
  2.7 0.2 select_reduce_fusion
  2.9 0.6 pad_maximum_fusion.3.levels_s
  3.5 0.1 fusion.7
  3.6 0.0 copy-done.1
  3.7 0.0 copy-done.3
  3.7 0.0 copy-start.2
  3.7 0.4 fusion.3
  4.0 0.0 copy-done
  4.0 0.0 copy-done.4
  4.0 0.0 copy-done.5
  4.0 0.5 fusion.20
  4.6 0.7 reshape.58.part_h
  5.3 0.5 copy.20
  5.8 1.1 reshape.59.stale_h
  6.9 104.5 %shard_map.136 = bf16[384,1152]{1,0:T(8,128)(2,1)} custom-call(f32[6]{0:T(128)} %pad_maximum_fusion.3.levels_s, f32[3,4,4,32]{3,2,1,0:T(4,128)} %bitcast.30, f32[3,4,16,64]{3,2,1,0:T(8,128)} %bitcast.29, f32[16,1152]{1,0:T(8,128)} %embed_h.1, f32[256,1152]{1,0:T(8,128)} %bitcast.22, f32[8,4096]{1,0:T(8,128)} %reshape.58.part_h, ...), custom_call_target="tpu_custom_call" | custom-call | tf_op jit(solution)/shard_map/pallas_call | solution.py:615
  111.4 2.2 %copy.22 = bf16[3,4,32,1152]{3,2,1,0:T(8,128)(2,1)} copy(bf16[3,4,32,1152]{3,2,1,0:T(8,128)(2,1)} %bitcast.24) | data formatting | bytes 1769472
  (12 shorter events, 0.2 us)
Async XLA Ops:
  0.0 4.0 %copy-start = (bf16[72,6912]{1,0:T(8,128)(2,1)S(1)}, bf16[72,6912]{1,0:T(8,128)(2,1)}, u32[]{:S(2)}) copy-start(bf16[72,6912]{1,0:T(8,128)(2,1)} %param.23) | copy-start | bytes 2985988
  0.8 1.9 %copy-start.6 = (s32[3]{0:T(128)S(1)}, s32[3]{0:T(128)}, u32[]{:S(2)}) copy-start(s32[3]{0:T(128)} %param.16) | copy-start | bytes 40
  0.8 2.8 %copy-start.1 = (bf16[256,1152]{1,0:T(8,128)(2,1)S(1)}, bf16[256,1152]{1,0:T(8,128)(2,1)}, u32[]{:S(2)}) copy-start(bf16[256,1152]{1,0:T(8,128)(2,1)} %param.20) | copy-start | bytes 1769476
  0.8 2.8 %copy-start.3 = (bf16[1152,72]{0,1:T(8,128)(2,1)S(1)}, bf16[1152,72]{0,1:T(8,128)(2,1)}, u32[]{:S(2)}) copy-start(bf16[1152,72]{0,1:T(8,128)(2,1)} %param.21) | copy-start | bytes 497668
  0.8 3.2 %copy-start.4 = (bf16[1001,72]{0,1:T(8,128)(2,1)S(1)}, bf16[1001,72]{0,1:T(8,128)(2,1)}, u32[]{:S(2)}) copy-start(bf16[1001,72]{0,1:T(8,128)(2,1)} %param.22) | copy-start | bytes 432436
  0.9 3.2 %copy-start.5 = (s32[3]{0:T(128)S(1)}, s32[3]{0:T(128)}, u32[]{:S(2)}) copy-start(s32[3]{0:T(128)} %param.17) | copy-start | bytes 40
  3.7 1.6 %copy-start.2 = (bf16[2,3,2,32,576]{4,3,2,1,0:T(8,128)(2,1)S(1)}, bf16[2,3,2,32,576]{4,3,2,1,0:T(8,128)(2,1)}, u32[]{:S(2)}) copy-start(bf16[2,3,2,32,576]{4,3,2,1,0:T(8,128)(2,1)} %param.18) | copy-start | bytes 1327108

commit v3 on v2

v3 whole, which is shorter than its diff:
```python
import math

import jax
import jax.numpy as jnp
from jax import lax
from jax.experimental import pallas as pl
from jax.experimental.pallas import tpu as pltpu
from jax.sharding import PartitionSpec as P

HD = 72
TSTEPS = 1000


def fused_block(t_index, labels, x_lo, noise, embed, tw1, tw2, table, ada, stale, wqkv, ow, fc1, fc2):
    D = 1152
    L2E = 1.4426950408889634
    QS = L2E / math.sqrt(HD)
    bf, f32 = jnp.bfloat16, jnp.float32
    NKEY = 256 + 15 * 64
    HID = 4608
    UNROLL = 2
    EARLY = 256 + 9 * 64

    def kernel(
        t_s, label_s, x_h, noise_h, embed_h, tw1_h, tw2_h, table_h, ada_h, stale_h, wqkv_h, ow_h, fc1_h,
        fc2_h, out_ref, xn, nz, emb, pos, tw1, tw2, table, ada, skv, kown, att1, mass1, part, rsb, both_ref, gs, modp, noisy,
        tok, wq, kvb, wb, owb, qb, att, attr, n2, mid, acc, send, recv, local,
    ):
        row, col, head = lax.axis_index("row"), lax.axis_index("col"), lax.axis_index("head")
        z, core = row // 2, row % 2
        x, y = head * 2 + col // 4, col % 4

        def at(x_, y_, z_, core_):
            return (z_ * 2 + core_, (x_ % 2) * 4 + y_, x_ // 2)

        peers = {
            "sib": at(x, y, z, 1 - core),
            "zp": at(x, y, (z + 1) % 8, core),
            "zm": at(x, y, (z + 7) % 8, core),
            "ap": at((x + core) % 4, (y + 1 - core) % 4, z, core),
            "am": at((x + 4 - core) % 4, (y + 3 + core) % 4, z, core),
            "bp": at((x + 1 - core) % 4, (y + core) % 4, z, core),
            "bm": at((x + 3 + core) % 4, (y + 4 - core) % 4, z, core),
            "far": at((x + 2) % 4, y, z, core),
        }
        other = at(3 - x, y, z, core)
        twin = at(x, y, z + 1 - 2 * (z % 2), core)
        near = {}
        for dr in (1, 15):
            near[f"h{dr}"] = ((row + dr) % 16, col, 1 - head)
        fellows = {k: ((row + k) % 16, col, head) for k in range(1, 16)}

        copies = {}
        order = {"n": 0}

        def remote(name, src, dst, peer):
            k = order["n"]
            order["n"] = k + 1
            c = pltpu.make_async_remote_copy(
                src_ref=src, dst_ref=dst, send_sem=send.at[k], recv_sem=recv.at[k],
                device_id=peer, device_id_type=pl.DeviceIdType.MESH,
            )
            copies[name] = c
            return c

        def go(name):
            copies[name].start()

        def got(name):
            copies[name].wait_recv()

        loads = []

        def load(src, dst):
            c = pltpu.make_async_copy(src, dst, local.at[len(loads)])
            loads.append(c)
            c.start()
            return c

        SIZE, PLUS, LIFT = {"": 112, "E": 32}, {"": 64, "E": 16}, {"": 0, "E": 448}

        def blk(kind, group, j, part=None):
            lo, n = {
                None: (0, SIZE[kind]), 0: (0, PLUS[kind]), 1: (PLUS[kind], SIZE[kind] - PLUS[kind])
            }[part]
            return wb.at[:, pl.ds(group * 1152 + LIFT[kind] + j * SIZE[kind] + lo, n), :]

        def ring(tag, sides, place):
            p, m = sides
            remote(tag + "1", place(0, None), place(1, None), p)
            remote(tag + "2", place(0, None), place(2, None), m)
            remote(tag + "3a", place(1, 0), place(3, 0), p)
            remote(tag + "3b", place(2, 1), place(3, 1), m)

        along = {
            "A": (peers["ap"], peers["am"]),
            "B": (peers["bp"], peers["bm"]),
            "EA": (at((x + 1) % 4, y, z, core), at((x + 3) % 4, y, z, core)),
            "EB": (at(x, (y + 1) % 4, z, core), at(x, (y + 3) % 4, z, core)),
        }
        for kind in ("", "E"):
            ring(kind + "A", along[kind + "A"], lambda g, part, kind=kind: blk(kind, g, 0, part))
            for g in range(4):
                ring(
                    f"{kind}B{g}", along[kind + "B"],
                    lambda j, part, g=g, kind=kind: blk(kind, g, j, part),
                )
        for name, lo, n in [(f"S{g}", g * 1152, 576) for g in range(3)] + [
            ("S3m", 3456, 336), ("S3e", 3904, 96), ("S3mz", 3792, 112), ("S3ez", 4000, 32)
        ]:
            remote(name, wb.at[:, pl.ds(lo, n), :], wb.at[:, pl.ds(lo + 576, n), :], peers["sib"])

        def slot(b, s, lo=0, n=64):
            return kvb.at[b, pl.ds(256 + s * 64 + lo, n), :]

        for b in range(3):
            own = kown.at[b]
            zp, zm = peers["zp"], peers["zm"]
            right, left = (0, 2, 9), (1, 3, 10)
            remote(f"R1_{b}", own, slot(b, 0), zp)
            remote(f"L1_{b}", own, slot(b, 1), zm)
            for d in (1, 2):
                remote(f"R{d + 1}_{b}", slot(b, right[d - 1]), slot(b, right[d]), zp)
                remote(f"L{d + 1}_{b}", slot(b, left[d - 1]), slot(b, left[d]), zm)
            remote(f"R4_{b}", slot(b, 9, 0, 32), slot(b, 11, 0, 32), zp)
            remote(f"L4_{b}", slot(b, 10, 32, 32), slot(b, 11, 32, 32), zm)
            remote(f"C0_{b}", own, slot(b, 4), peers["sib"])
            remote(f"C1_{b}", slot(b, 0, 0, 256), slot(b, 5, 0, 256), peers["sib"])
            remote(f"C2_{b}", slot(b, 9, 0, 192), slot(b, 12, 0, 192), peers["sib"])
            remote(
                f"X{b}", att.at[b, :, 1 - head], attr.at[b], peers["far"],
            )
        part_at = lambda p: p * 288 + core * 144
        ow_own = pl.ds(pl.multiple_of(part_at(z % 2), 16), 144)
        far0 = pl.ds(pl.multiple_of(704 + part_at(z % 2), 16), 144)
        far1 = pl.ds(pl.multiple_of(704 + part_at(1 - z % 2), 16), 144)
        remote("O", ow_h.at[ow_own, :], owb.at[far0, :], other)
        remote("OZ", owb.at[far0, :], owb.at[far0, :], twin)
        remote("OS0", owb.at[far0, :], owb.at[far0, :], peers["sib"])
        remote("OS1", owb.at[far1, :], owb.at[far1, :], peers["sib"])
        remote("Pf", xn.at[1, head], xn.at[1, head], peers["far"])
        remote("Pd", xn.at[1, head], xn.at[0, head], fellows[1])
        remote("Pu", xn.at[1, head], xn.at[2, head], fellows[15])
        remote("Pdf", xn.at[1, head], xn.at[0, head], near["h1"])
        remote("Puf", xn.at[1, head], xn.at[2, head], near["h15"])
        for k in range(1, 16):
            to = (row + k) % 16
            chunk = pl.ds(pl.multiple_of(to * 256, 256), 256)
            remote(f"M{k}", part.at[:, chunk], rsb.at[k], fellows[k])
            remote(f"G{k}", both_ref, gs.at[row], fellows[k])

        c_w = []
        for kind, lo in (("", 0), ("E", 112)):
            rows = pl.ds(pl.multiple_of(core * 144 + lo, 16), SIZE[kind])
            for k, w_h in enumerate((fc1_h, fc2_h)):
                c_w.append(load(w_h.at[rows, :], wb.at[k, pl.ds(LIFT[kind], SIZE[kind]), :]))
        c_x = load(x_h, xn.at[1, head])
        c_tw1 = load(tw1_h, tw1)
        c_tw2 = load(tw2_h, tw2)
        c_table = load(table_h, table)
        c_ada = load(ada_h, ada)
        c_skv = load(stale_h, skv)
        c_nz = load(noise_h, nz)
        c_emb = load(embed_h, emb)
        c_wq = load(wqkv_h, wq)
        c_ow = load(ow_h, owb.at[pl.ds(64, 576), :])
        barrier = pltpu.get_barrier_semaphore()
        greet = list(fellows.values()) + list(near.values())
        greet += [peers[n] for n in ("ap", "am", "bp", "bm", "far")]
        for peer in greet:
            pl.semaphore_signal(barrier, inc=1, device_id=peer, device_id_type=pl.DeviceIdType.MESH)
        owb[pl.ds(0, 64), :] = jnp.zeros((64, D), bf)
        owb[pl.ds(640, 64), :] = jnp.zeros((64, D), bf)
        att[...] = jnp.zeros_like(att)
        att1[...] = jnp.zeros_like(att1)
        mass1[...] = jnp.zeros_like(mass1)
        acc[...] = jnp.zeros_like(acc)
        c_skv.wait()
        for b in range(3):
            kown[b] = jnp.concatenate([skv[0, b], skv[1, b]], axis=-1).reshape(64, D)
        def by_image(values, shape):
            r = lax.broadcasted_iota(jnp.int32, shape, 0)
            return jnp.where(r == 0, values[0], jnp.where(r == 1, values[1], values[2]))

        ts = [t_s[b] for b in range(3)]
        k128 = lax.broadcasted_iota(jnp.int32, (8, 128), 1).astype(f32)
        angles = by_image(ts, (8, 128)).astype(f32) * jnp.exp(-math.log(10000.0) * k128 / 128)
        feats = jnp.concatenate([jnp.cos(angles), jnp.sin(angles)], axis=1).astype(bf)
        c_tw1.wait()
        hid = jnp.dot(feats, tw1[...], preferred_element_type=f32)
        hid = (hid * jax.nn.sigmoid(hid)).astype(bf)
        c_tw2.wait()
        c_table.wait()
        NT = (((1,), (1,)), ((), ()))
        kinds = lax.broadcasted_iota(jnp.int32, (8, 1001), 1)
        picked = kinds == by_image([label_s[b] for b in range(3)], (8, 1001))
        cond = lax.dot_general(hid, tw2[...], NT, preferred_element_type=f32)
        cond = cond + lax.dot_general(
            picked.astype(f32).astype(bf), table[...], NT, preferred_element_type=f32
        )
        cond = (cond * jax.nn.sigmoid(cond)).astype(bf)
        c_ada.wait()
        for k in range(2):
            first = jnp.dot(cond, ada[:, pl.ds(k * 3 * D, 3 * D)], preferred_element_type=f32)
            part[pl.ds(4 * k, 4), pl.ds(0, 3 * D)] = first[0:4]
        steps = lax.broadcasted_iota(jnp.int32, (8, TSTEPS), 1)
        betas = 0.0001 + (0.02 - 0.0001) * steps.astype(f32) / (TSTEPS - 1)
        logs = jnp.where(steps <= by_image(ts, (8, TSTEPS)), jnp.log(1.0 - betas), 0.0)
        abar = jnp.exp(jnp.sum(logs, axis=1, keepdims=True))

        def wide(column):
            return jnp.stack([jnp.broadcast_to(column[b : b + 1], (4, 64)) for b in range(3)])

        keep, fuzz = wide(jnp.sqrt(abar)), wide(jnp.sqrt(1.0 - abar))

        def waves(n, start):
            place = (lax.broadcasted_iota(jnp.int32, (n, D // 4), 0) + start).astype(f32)
            k = lax.broadcasted_iota(jnp.int32, (n, D // 4), 1).astype(f32)
            args = place * jnp.exp(-math.log(10000.0) * k / (D // 4))
            return jnp.concatenate([jnp.sin(args), jnp.cos(args)], axis=1)

        rp, cp = waves(8, row * 4), waves(64, 0)
        for i in range(4):
            pos[pl.ds(i * 64, 64), :] = jnp.concatenate(
                [jnp.broadcast_to(rp[i : i + 1], (64, D // 2)), cp], axis=1
            )
        c_x.wait()
        pl.semaphore_wait(barrier, len(greet))
        for n in ("Pf", "Pd", "Pu", "Pdf", "Puf"):
            go(n)
        for k in range(1, 16):
            go(f"M{k}")
        go("R1_0")
        go("L1_0")
        for c in c_w:
            c.wait()
        for n in ("A1", "A2", "EA1", "EA2", "B01", "B02", "EB01", "EB02"):
            go(n)
        for b in range(3):
            go(f"C0_{b}")
        c_nz.wait()
        c_emb.wait()
        for n in ("Pf", "Pd", "Pu", "Pdf", "Puf"):
            got(n)

        def line(d, i):
            return jnp.concatenate([xn[d, 0, :, i], xn[d, 1, :, i]], axis=-1)

        lines = [line(0, 3)] + [line(1, i) for i in range(4)] + [line(2, 0)]
        lines[0] = jnp.where(row == 0, lines[1], lines[0])
        lines[5] = jnp.where(row == 15, lines[4], lines[5])
        total = jnp.zeros((3, 4, 64), f32)
        square = jnp.zeros((3, 4, 64), f32)
        for i in range(4):
            for di in range(2):
                v = 0.75 * lines[i + 1] + 0.25 * lines[i + 2 * di]
                sides = (
                    jnp.concatenate([v[:, :, :1], v[:, :, :63]], axis=-1),
                    jnp.concatenate([v[:, :, 1:], v[:, :, 63:]], axis=-1),
                )
                for dj in range(2):
                    k = 2 * di + dj
                    n = keep * (0.75 * v + 0.25 * sides[dj]) + fuzz * nz[:, i, 4 * k : 4 * k + 4, :]
                    noisy[:, i, 4 * k : 4 * k + 4, :] = n
                    total = total + n
                    square = square + n * n
        lane1 = lax.broadcasted_iota(jnp.int32, (8, 128), 1)
        both = jnp.zeros((8, 128), f32)
        for b in range(3):
            s = jnp.concatenate(
                [
                    jnp.sum(total[b], axis=1, keepdims=True),
                    jnp.sum(square[b], axis=1, keepdims=True),
                ],
                axis=0,
            )
            both = jnp.where(lane1 == b, jnp.broadcast_to(s, (8, 128)), both)
        both_ref[:, pl.ds(256, 128)] = both
        for k in range(1, 16):
            got(f"M{k}")
        mine = pl.ds(pl.multiple_of(row * 256, 256), 256)
        piece = part[:, mine]
        for k in range(1, 16):
            piece = piece + rsb[k]
        both_ref[:, pl.ds(0, 256)] = piece
        gs[row] = jnp.concatenate([piece, both], axis=1)
        for k in range(1, 16):
            go(f"G{k}")
        for b in (1, 2):
            go(f"R1_{b}")
            go(f"L1_{b}")

        def norm(v):
            centre = jnp.mean(v, axis=-1, keepdims=True)
            v = v - centre
            spread = jnp.mean(v * v, axis=-1, keepdims=True)
            return v * lax.rsqrt(spread + 1e-06)

        def modrow(b, k):
            return modp[pl.ds(b + 4 * (k // 3), 1), pl.ds((k % 3) * D, D)]

        def qkv(b):
            n1 = (
                norm(tok[b].reshape(256, D).astype(f32)) * (1.0 + modrow(b, 1)) + modrow(b, 0)
            ).astype(bf)
            q = lax.dot_general(n1, wq[pl.ds(0, 576), :], NT, preferred_element_type=f32)
            qb[b, :, pl.ds(0, 576)] = (q * QS).astype(bf)
            kv = lax.dot_general(n1, wq[pl.ds(576, 1152), :], NT, preferred_element_type=f32)
            kvb[b, pl.ds(0, 256), :] = kv.astype(bf)

        lane = lax.broadcasted_iota(jnp.int32, (1, 256), 1)

        lane128 = lax.broadcasted_iota(jnp.int32, (1, 128), 1)

        def attend(b, late):
            keys = pl.ds(EARLY, NKEY - EARLY) if late else pl.ds(0, EARLY)

            def score(h):
                first = h * HD
                ks = pl.multiple_of((first // 128) * 128, 128)
                off = first - ks
                here = (lane >= off) & (lane < off + HD)
                q = qb[b, :, pl.ds(ks, 256)]
                q = jnp.where(here, q, jnp.zeros_like(q))
                return lax.dot_general(
                    q, kvb[b, keys, pl.ds(ks, 256)], NT, preferred_element_type=f32
                )

            def mix(h, s):
                first = h * HD
                vs = pl.multiple_of(jnp.minimum(((576 + first) // 128) * 128, 896), 128)
                voff = 576 + first - vs
                mine = (lane >= voff) & (lane < voff + HD)
                cols = pl.ds(pl.multiple_of(vs - 512, 128), 256)
                chosen = lane128 == h
                if late:
                    top = jnp.max(s, axis=1, keepdims=True) + 2.0
                    before = jnp.sum(jnp.where(chosen, mass1[b], 0.0), axis=1, keepdims=True)
                    top = jnp.maximum(top, before)
                    p = jnp.exp2(s - (top - 2.0))
                    kept = jnp.exp2(before - top)
                    mass = jnp.sum(p, axis=1, keepdims=True) + kept
                    o = jnp.dot(p.astype(bf), kvb[b, keys, pl.ds(vs, 256)], preferred_element_type=f32)
                    o = (o + kept * att1[b, :, cols]) * (1.0 / mass)
                    o = o.astype(bf).reshape(4, 2, 32, 256)
                    att[b, :, :, :, cols] = jnp.where(
                        mine.reshape(1, 1, 1, 256), o, att[b, :, :, :, cols]
                    )
                    return
                fresh, old = s[:, :256], s[:, 256:]
                top = jnp.maximum(
                    jnp.max(fresh, axis=1, keepdims=True), jnp.max(old, axis=1, keepdims=True) + 2.0
                )
                p0 = jnp.exp2(fresh - top)
                p1 = jnp.exp2(old - (top - 2.0))
                mass = jnp.sum(p0, axis=1, keepdims=True) + jnp.sum(p1, axis=1, keepdims=True)
                o = jnp.dot(
                    p0.astype(bf), kvb[b, pl.ds(0, 256), pl.ds(vs, 256)],
                    preferred_element_type=f32,
                ) + jnp.dot(
                    p1.astype(bf), kvb[b, pl.ds(256, EARLY - 256), pl.ds(vs, 256)],
                    preferred_element_type=f32,
                )
                att1[b, :, cols] = jnp.where(mine, o * (1.0 / mass), att1[b, :, cols])
                mass1[b] = jnp.where(chosen, top + jnp.log2(mass), mass1[b])

            def some(i, _):
                hs = [i * UNROLL + j for j in range(UNROLL)]
                ss = [score(h) for h in hs]
                for h, s in zip(hs, ss):
                    mix(h, s)
                return 0

            lax.fori_loop(0, 8 // UNROLL, some, 0)

        def project(b):
            mine = att[b, :, head].reshape(128, 640)
            p = jnp.dot(mine, owb[pl.ds(0, 640), :], preferred_element_type=f32)
            p = p + jnp.dot(attr[b].reshape(128, 640), owb[pl.ds(640, 640), :], preferred_element_type=f32)
            t = tok[b, :, head].reshape(128, D).astype(f32)
            m = (t + modrow(b, 2) * p).astype(bf)
            mid[pl.ds(b * 128, 128), :] = m
            n = norm(m.astype(f32)) * (1.0 + modrow(b, 4)) + modrow(b, 3)
            n2[pl.ds(b * 128, 128), :] = n.astype(bf)

        def feed(first, count):
            def one(i, _):
                r = pl.ds(pl.multiple_of(first + i * 768, 256), 768)
                hid = lax.dot_general(n2[...], wb[0, r, :], NT, preferred_element_type=f32)
                hid = jax.nn.gelu(hid, approximate=True).astype(bf)
                acc[...] += jnp.dot(hid, wb[1, r, :], preferred_element_type=f32)
                return 0

            lax.fori_loop(0, count, one, 0)

        def kstep(d, b):
            got(f"R{d}_{b}")
            got(f"L{d}_{b}")
            if d < 4:
                go(f"R{d + 1}_{b}")
                go(f"L{d + 1}_{b}")

        def fwd(tag):
            got(tag + "1")
            go(tag + "3a")
            got(tag + "2")
            go(tag + "3b")

        def done(tag):
            got(tag + "3a")
            got(tag + "3b")

        kstep(1, 0)
        for k in range(1, 16):
            got(f"G{k}")
        both = jnp.zeros((8, 128), f32)
        for r in range(16):
            both = both + gs[r, :, pl.ds(256, 128)]
            modp[:, pl.ds(r * 256, 256)] = gs[r, :, pl.ds(0, 256)]
        shares, gains = [], []
        for b in range(3):
            col_b = jnp.sum(jnp.where(lane1 == b, both, 0.0), axis=1, keepdims=True) / 16384.0
            centre = col_b[0:4]
            gain = lax.rsqrt(col_b[4:8] - centre * centre + 1e-05)
            shares.append(jnp.concatenate([centre] * 4, axis=0))
            gains.append(jnp.concatenate([gain] * 4, axis=0))
        whi = emb[...].astype(bf)
        wlo = (emb[...] - whi.astype(f32)).astype(bf)
        w3 = jnp.concatenate([whi, whi, wlo], axis=0)
        c_wq.wait()
        for b in range(3):
            for i in range(4):
                n = (noisy[b, i] - shares[b]) * gains[b]
                hi = n.astype(bf)
                lo = (n - hi.astype(f32)).astype(bf)
                e = lax.dot_general(
                    jnp.concatenate([hi, lo, hi], axis=0), w3, (((0,), (0,)), ((), ())),
                    preferred_element_type=f32,
                )
                e = (e + pos[pl.ds(i * 64, 64), :]).astype(bf)
                tok[b, i] = e.reshape(2, 32, D)
        def both_kinds(act, tag):
            act(tag)
            act("E" + tag)

        def begin(tag):
            go(tag + "1")
            go(tag + "2")

        both_kinds(fwd, "A")
        for g in (1, 2):
            both_kinds(begin, f"B{g}")
        go("O")
        kstep(1, 1)
        qkv(0)
        kstep(1, 2)
        qkv(1)
        kstep(2, 0)
        go("C1_0")
        both_kinds(fwd, "B0")
        qkv(2)
        kstep(2, 1)
        go("C1_1")
        got("C0_0")
        got("C1_0")
        attend(0, False)
        kstep(2, 2)
        go("C1_2")
        both_kinds(done, "A")
        both_kinds(begin, "B3")
        got("C0_1")
        got("C1_1")
        kstep(3, 0)
        attend(1, False)
        kstep(3, 1)
        got("C0_2")
        got("C1_2")
        got("O")
        go("OS0")
        attend(2, False)
        kstep(3, 2)
        kstep(4, 0)
        go("C2_0")
        both_kinds(fwd, "B1")
        kstep(4, 1)
        go("C2_1")
        got("C2_0")
        attend(0, True)
        go("X0")
        kstep(4, 2)
        go("C2_2")
        go("OZ")
        got("C2_1")
        attend(1, True)
        go("X1")
        both_kinds(done, "B0")
        go("S0")
        got("C2_2")
        attend(2, True)
        go("X2")
        both_kinds(fwd, "B2")
        got("OZ")
        go("OS1")
        c_ow.wait()
        got("OS0")
        got("X0")
        got("OS1")
        project(0)
        both_kinds(fwd, "B3")
        go("S3m")
        go("S3e")
        got("X1")
        project(1)
        got("X2")
        project(2)
        got("S0")
        feed(0, 1)
        both_kinds(done, "B1")
        go("S1")
        both_kinds(done, "B2")
        go("S2")
        got("S1")
        feed(768, 2)
        both_kinds(done, "B3")
        go("S3mz")
        go("S3ez")
        got("S2")
        feed(2304, 1)
        got("S3m")
        feed(3072, 1)
        got("S3e")
        got("S3mz")
        got("S3ez")
        feed(3840, 1)
        for b in range(3):
            r = pl.ds(b * 128, 128)
            out_ref[r, :] = (mid[r, :].astype(f32) + modrow(b, 5) * acc[r, :]).astype(bf)
        for c in copies.values():
            c.wait_send()

    any_spec = pl.BlockSpec(memory_space=pl.ANY)
    n_copies = 2 * 20 + 7 + 3 * 12 + 4 + 5 + 30
    return pl.pallas_call(
        kernel,
        out_shape=jax.ShapeDtypeStruct((384, D), bf),
        in_specs=[pl.BlockSpec(memory_space=pltpu.SMEM)] * 2 + [any_spec] * 12,
        out_specs=pl.BlockSpec(memory_space=pltpu.VMEM),
        scratch_shapes=[
            pltpu.VMEM((3, 2, 3, 4, 4, 32), f32),
            pltpu.VMEM((3, 4, 16, 64), f32),
            pltpu.VMEM((16, D), f32),
            pltpu.VMEM((256, D), f32),
            pltpu.VMEM((256, D), bf),
            pltpu.VMEM((72, D), bf),
            pltpu.VMEM((72, 1001), bf),
            pltpu.VMEM((72, 6 * D), bf),
            pltpu.VMEM((2, 3, 2, 32, 576), bf),
            pltpu.VMEM((3, 64, D), bf),
            pltpu.VMEM((3, 256, 640), f32),
            pltpu.VMEM((3, 256, 128), f32),
            pltpu.VMEM((8, 4096), f32),
            pltpu.VMEM((16, 8, 256), f32),
            pltpu.VMEM((8, 384), f32),
            pltpu.VMEM((16, 8, 384), f32),
            pltpu.VMEM((8, 4096), f32),
            pltpu.VMEM((3, 4, 16, 64), f32),
            pltpu.VMEM((3, 4, 2, 32, D), bf),
            pltpu.VMEM((1728, D), bf),
            pltpu.VMEM((3, NKEY, D), bf),
            pltpu.VMEM((2, HID, D), bf),
            pltpu.VMEM((1280, D), bf),
            pltpu.VMEM((3, 256, 640), bf),
            pltpu.VMEM((3, 4, 2, 32, 640), bf),
            pltpu.VMEM((3, 4, 32, 640), bf),
            pltpu.VMEM((384, D), bf),
            pltpu.VMEM((384, D), bf),
            pltpu.VMEM((384, D), f32),
            pltpu.SemaphoreType.DMA((n_copies,)),
            pltpu.SemaphoreType.DMA((n_copies,)),
            pltpu.SemaphoreType.DMA((14,)),
        ],
        compiler_params=pltpu.CompilerParams(
            collective_id=0, has_side_effects=True, vmem_limit_bytes=64_000_000
        ),
    )(t_index, labels, x_lo, noise, embed, tw1, tw2, table, ada, stale, wqkv, ow, fc1, fc2)


def body(
    x_lo,
    noise,
    t_index,
    labels,
    stale_kv,
    embed_w,
    t_w1,
    t_w2,
    class_table,
    ada_w,
    qkv_w,
    out_w,
    fc1_w,
    fc2_w,
):
    head_count = lax.axis_size("head")
    tile_rows, full_cols = noise.shape[1], noise.shape[2]
    batch, width = noise.shape[0], embed_w.shape[1]
    half = full_cols // head_count
    local_width = qkv_w.shape[2]
    out = fused_block(
        t_index,
        labels,
        x_lo.transpose(0, 1, 3, 2),
        noise.transpose(0, 1, 3, 2),
        embed_w,
        t_w1,
        t_w2.T,
        class_table.T,
        ada_w,
        stale_kv,
        qkv_w.transpose(1, 2, 0).reshape(3 * local_width, width),
        out_w,
        fc1_w.T,
        fc2_w.T,
    )
    return out.reshape(batch, tile_rows, half, width)


def solution(mesh):
    placed = (
        P("col", "row", "head", None),
        P("col", "row", None, None),
        P("col"),
        P("col"),
        P(None, "col", "row", None, "head"),
        P(),
        P(),
        P(None, "row"),
        P(None, "row"),
        P("row", None),
        P(None, None, "head"),
        P("head", None),
        P(None, ("col", "head")),
        P(None, ("col", "head")),
    )
    return jax.shard_map(
        body, mesh=mesh, in_specs=placed, out_specs=P("col", "row", "head", None), check_vma=False
    )
```

time: 114 us -> 96.7 us (0.85)
  Pallas kernels: 105 us -> 94.4 us
  other arithmetic: 3.23 us -> 0 us
  local copies, waits for them, and re-layouts: 4.84 us -> 2.17 us
    pallas_call x1, Pallas kernels: 105 us -> 94.4 us  [fused_block(): pl.pallas_call(kernel, out_shape=jax.ShapeDtypeStruct((384, D), bf), in_s...]
    concatenate x4 -> x0, other arithmetic: 2 us -> none  [the longest x1 1.25 us: position_table(): jnp.concatenate([jnp.broadcast_to(row_part[:, None, :], (n_rows, n_cols,...]
    reshape x3 -> x0, local copies, waits for them, and re-layouts: 1.82 us -> none  [the longest x1 1.11 us: body(): stale_kv.transpose(1, 2, 3, 0, 4).reshape(batch, -1, 2 * local_width)]
where the time goes in v3:
time: 96.7 us; the launch traced here: 96.6 us
  Pallas kernels  94.4 us (98%)
  local copies, waits for them, and re-layouts  2.17 us (2%)
    pallas_call x1, Pallas kernels, fused_block(): pl.pallas_call(kernel, out_shape=jax.ShapeDtypeStruct((384, D), bf), in_s...  94.4 us
    unnamed x1, local copies, waits for them, and re-layouts  2.17 us

profile of v3, /device:TPU:1, one launch (start us, length us, event | category | flops | bytes accessed | tf_op | source)
XLA Modules:
  0.0 96.6 jit_solution(14093844850119135715)
XLA Ops:
  0.0 94.4 %shard_map.136 = bf16[384,1152]{1,0:T(8,128)(2,1)} custom-call(s32[3]{0:T(128)} %t_s.1, s32[3]{0:T(128)} %label_s.1, f32[3,4,4,32]{3,2,1,0:T(4,128)} %bitcast.17, f32[3,4,16,64]{3,2,1,0:T(8,128)} %bitcast.16, f32[16,1152]{1,0:T(8,128)} %embed_h.1, bf16[256,1152]{1,0:T(8,128)(2,1)} %tw1_h.1, bf16[72,1152]{1,0:T(8,128)(2,1)} %bitcast.14, ...), custom_call_target="tpu_custom_call" | custom-call | tf_op jit(solution)/shard_map/pallas_call | solution.py:543
  94.4 2.2 %copy.16 = bf16[3,4,32,1152]{3,2,1,0:T(8,128)(2,1)} copy(bf16[3,4,32,1152]{3,2,1,0:T(8,128)(2,1)} %bitcast.11) | data formatting | bytes 1769472

commit v4 on v3

--- a/solution.py
+++ b/solution.py
@@ -23,8 +23,8 @@
 
     def kernel(
         t_s, label_s, x_h, noise_h, embed_h, tw1_h, tw2_h, table_h, ada_h, stale_h, wqkv_h, ow_h, fc1_h,
-        fc2_h, out_ref, xn, nz, emb, pos, tw1, tw2, table, ada, skv, kown, att1, mass1, part, rsb, both_ref, gs, modp, noisy,
-        tok, wq, kvb, wb, owb, qb, att, attr, n2, mid, acc, send, recv, local,
+        fc2_h, out_ref, xn, nz, emb, pos, tw1, tw2, table, ada, skv, kown, att1, mass1, part, pieces, rsb, both_ref, gs, modp, noisy,
+        tok, wq, kvb, wb, owb, qb, att, attr, n2, mid, acc, outb, send, recv, local,
     ):
         row, col, head = lax.axis_index("row"), lax.axis_index("col"), lax.axis_index("head")
         z, core = row // 2, row % 2
@@ -77,13 +77,17 @@
             c.start()
             return c
 
-        SIZE, PLUS, LIFT = {"": 112, "E": 32}, {"": 64, "E": 16}, {"": 0, "E": 448}
+        SIZE, PLUS = {"": 112, "E": 32}, {"": 64, "E": 16}
 
         def blk(kind, group, j, part=None):
             lo, n = {
                 None: (0, SIZE[kind]), 0: (0, PLUS[kind]), 1: (PLUS[kind], SIZE[kind] - PLUS[kind])
             }[part]
-            return wb.at[:, pl.ds(group * 1152 + LIFT[kind] + j * SIZE[kind] + lo, n), :]
+            if j < 3:
+                base = group * 864 + (336 if kind else 0) + j * SIZE[kind]
+            else:
+                base = 3456 + group * 288 + (112 if kind else 0)
+            return wb.at[:, pl.ds(base + lo, n), :]
 
         def ring(tag, sides, place):
             p, m = sides
@@ -105,10 +109,11 @@
                     f"{kind}B{g}", along[kind + "B"],
                     lambda j, part, g=g, kind=kind: blk(kind, g, j, part),
                 )
-        for name, lo, n in [(f"S{g}", g * 1152, 576) for g in range(3)] + [
-            ("S3m", 3456, 336), ("S3e", 3904, 96), ("S3mz", 3792, 112), ("S3ez", 4000, 32)
-        ]:
-            remote(name, wb.at[:, pl.ds(lo, n), :], wb.at[:, pl.ds(lo + 576, n), :], peers["sib"])
+        for g in range(4):
+            for name, lo, n in ((f"S{g}a", g * 864, 432), (f"S{g}b", 3456 + g * 288, 144)):
+                remote(
+                    name, wb.at[:, pl.ds(lo, n), :], wb.at[:, pl.ds(lo + n, n), :], peers["sib"]
+                )
 
         def slot(b, s, lo=0, n=64):
             return kvb.at[b, pl.ds(256 + s * 64 + lo, n), :]
@@ -143,17 +148,38 @@
         remote("Pu", xn.at[1, head], xn.at[2, head], fellows[15])
         remote("Pdf", xn.at[1, head], xn.at[0, head], near["h1"])
         remote("Puf", xn.at[1, head], xn.at[2, head], near["h15"])
+        shared = {}
+        for tag in "MG":
+            shared[tag] = order["n"]
+            order["n"] += 1
+        to_all = {"M": [], "G": []}
         for k in range(1, 16):
             to = (row + k) % 16
-            chunk = pl.ds(pl.multiple_of(to * 256, 256), 256)
-            remote(f"M{k}", part.at[:, chunk], rsb.at[k], fellows[k])
-            remote(f"G{k}", both_ref, gs.at[row], fellows[k])
+            chunk = pl.ds(pl.multiple_of(to * 128, 128), 128)
+            for tag, src, dst in (
+                ("M", pieces.at[:, chunk], rsb.at[k]), ("G", both_ref, gs.at[k])
+            ):
+                to_all[tag].append(
+                    pltpu.make_async_remote_copy(
+                        src_ref=src, dst_ref=dst, send_sem=send.at[shared[tag]],
+                        recv_sem=recv.at[shared[tag]], device_id=fellows[k],
+                        device_id_type=pl.DeviceIdType.MESH,
+                    )
+                )
+
+        def all15(tag):
+            buf = {"M": rsb, "G": gs}[tag].at[pl.ds(1, 15)]
+            return pltpu.make_async_remote_copy(
+                src_ref=buf, dst_ref=buf, send_sem=send.at[shared[tag]],
+                recv_sem=recv.at[shared[tag]], device_id=fellows[1],
+                device_id_type=pl.DeviceIdType.MESH,
+            )
 
         c_w = []
         for kind, lo in (("", 0), ("E", 112)):
             rows = pl.ds(pl.multiple_of(core * 144 + lo, 16), SIZE[kind])
             for k, w_h in enumerate((fc1_h, fc2_h)):
-                c_w.append(load(w_h.at[rows, :], wb.at[k, pl.ds(LIFT[kind], SIZE[kind]), :]))
+                c_w.append(load(w_h.at[rows, :], wb.at[k, pl.ds(336 if kind else 0, SIZE[kind]), :]))
         c_x = load(x_h, xn.at[1, head])
         c_tw1 = load(tw1_h, tw1)
         c_tw2 = load(tw2_h, tw2)
@@ -174,7 +200,6 @@
         att[...] = jnp.zeros_like(att)
         att1[...] = jnp.zeros_like(att1)
         mass1[...] = jnp.zeros_like(mass1)
-        acc[...] = jnp.zeros_like(acc)
         c_skv.wait()
         for b in range(3):
             kown[b] = jnp.concatenate([skv[0, b], skv[1, b]], axis=-1).reshape(64, D)
@@ -203,6 +228,10 @@
         for k in range(2):
             first = jnp.dot(cond, ada[:, pl.ds(k * 3 * D, 3 * D)], preferred_element_type=f32)
             part[pl.ds(4 * k, 4), pl.ds(0, 3 * D)] = first[0:4]
+        for r in range(16):
+            pieces[:, pl.ds(r * 128, 128)] = jnp.concatenate(
+                [part[:, pl.ds(r * 256, 128)], part[:, pl.ds(r * 256 + 128, 128)]], axis=0
+            ).astype(bf)
         steps = lax.broadcasted_iota(jnp.int32, (8, TSTEPS), 1)
         betas = 0.0001 + (0.02 - 0.0001) * steps.astype(f32) / (TSTEPS - 1)
         logs = jnp.where(steps <= by_image(ts, (8, TSTEPS)), jnp.log(1.0 - betas), 0.0)
@@ -228,13 +257,13 @@
         pl.semaphore_wait(barrier, len(greet))
         for n in ("Pf", "Pd", "Pu", "Pdf", "Puf"):
             go(n)
-        for k in range(1, 16):
-            go(f"M{k}")
+        for c in to_all["M"]:
+            c.start()
         go("R1_0")
         go("L1_0")
         for c in c_w:
             c.wait()
-        for n in ("A1", "A2", "EA1", "EA2", "B01", "B02", "EB01", "EB02"):
+        for n in ("A1", "A2", "EA1", "EA2", "O", "B01", "B02", "EB01", "EB02"):
             go(n)
         for b in range(3):
             go(f"C0_{b}")
@@ -265,7 +294,7 @@
                     total = total + n
                     square = square + n * n
         lane1 = lax.broadcasted_iota(jnp.int32, (8, 128), 1)
-        both = jnp.zeros((8, 128), f32)
+        head_mid = jnp.zeros((8, 128), f32), jnp.zeros((8, 128), f32)
         for b in range(3):
             s = jnp.concatenate(
                 [
@@ -274,18 +303,28 @@
                 ],
                 axis=0,
             )
-            both = jnp.where(lane1 == b, jnp.broadcast_to(s, (8, 128)), both)
-        both_ref[:, pl.ds(256, 128)] = both
+            s = jnp.broadcast_to(s, (8, 128))
+            s1 = s.astype(bf).astype(f32)
+            s2 = (s - s1).astype(bf).astype(f32)
+            s3 = s - s1 - s2
+            head_mid = (
+                jnp.where(lane1 == b, s1, jnp.where(lane1 == b + 3, s3, head_mid[0])),
+                jnp.where(lane1 == b, s2, head_mid[1]),
+            )
+        sums = jnp.concatenate(head_mid, axis=0).astype(bf)
+        both_ref[pl.ds(16, 16), :] = sums
+        all15("M").wait_recv()
+        at0 = pl.multiple_of(row * 256, 128)
+        piece = jnp.concatenate(
+            [part[:, pl.ds(at0, 128)], part[:, pl.ds(pl.multiple_of(at0 + 128, 128), 128)]], axis=0
+        )
         for k in range(1, 16):
-            got(f"M{k}")
-        mine = pl.ds(pl.multiple_of(row * 256, 256), 256)
-        piece = part[:, mine]
-        for k in range(1, 16):
-            piece = piece + rsb[k]
-        both_ref[:, pl.ds(0, 256)] = piece
-        gs[row] = jnp.concatenate([piece, both], axis=1)
-        for k in range(1, 16):
-            go(f"G{k}")
+            piece = piece + rsb[k].astype(f32)
+        piece = piece.astype(bf)
+        both_ref[pl.ds(0, 16), :] = piece
+        gs[0] = jnp.concatenate([piece, sums], axis=0)
+        for c in to_all["G"]:
+            c.start()
         for b in (1, 2):
             go(f"R1_{b}")
             go(f"L1_{b}")
@@ -374,24 +413,29 @@
             lax.fori_loop(0, 8 // UNROLL, some, 0)
 
         def project(b):
-            mine = att[b, :, head].reshape(128, 640)
-            p = jnp.dot(mine, owb[pl.ds(0, 640), :], preferred_element_type=f32)
-            p = p + jnp.dot(attr[b].reshape(128, 640), owb[pl.ds(640, 640), :], preferred_element_type=f32)
+            rows = pl.ds(b * 128, 128)
+            p = acc[rows, :] + jnp.dot(attr[b].reshape(128, 640), owb[pl.ds(640, 640), :], preferred_element_type=f32)
             t = tok[b, :, head].reshape(128, D).astype(f32)
             m = (t + modrow(b, 2) * p).astype(bf)
             mid[pl.ds(b * 128, 128), :] = m
             n = norm(m.astype(f32)) * (1.0 + modrow(b, 4)) + modrow(b, 3)
             n2[pl.ds(b * 128, 128), :] = n.astype(bf)
+            acc[rows, :] = jnp.zeros((128, D), f32)
+
+        def project_own(b):
+            mine = att[b, :, head].reshape(128, 640)
+            acc[pl.ds(b * 128, 128), :] = jnp.dot(
+                mine, owb[pl.ds(0, 640), :], preferred_element_type=f32
+            )
 
         def feed(first, count):
-            def one(i, _):
-                r = pl.ds(pl.multiple_of(first + i * 768, 256), 768)
-                hid = lax.dot_general(n2[...], wb[0, r, :], NT, preferred_element_type=f32)
+            rows = [pl.ds(first + i * 768, 768) for i in range(count)]
+            hids = [
+                lax.dot_general(n2[...], wb[0, r, :], NT, preferred_element_type=f32) for r in rows
+            ]
+            for r, hid in zip(rows, hids):
                 hid = jax.nn.gelu(hid, approximate=True).astype(bf)
                 acc[...] += jnp.dot(hid, wb[1, r, :], preferred_element_type=f32)
-                return 0
-
-            lax.fori_loop(0, count, one, 0)
 
         def kstep(d, b):
             got(f"R{d}_{b}")
@@ -411,15 +455,19 @@
             got(tag + "3b")
 
         kstep(1, 0)
-        for k in range(1, 16):
-            got(f"G{k}")
-        both = jnp.zeros((8, 128), f32)
-        for r in range(16):
-            both = both + gs[r, :, pl.ds(256, 128)]
-            modp[:, pl.ds(r * 256, 256)] = gs[r, :, pl.ds(0, 256)]
+        all15("G").wait_recv()
+        first, second = jnp.zeros((8, 128), f32), jnp.zeros((8, 128), f32)
+        for k in range(16):
+            g = gs[k].astype(f32)
+            first, second = first + g[16:24], second + g[24:32]
+            lo = pl.multiple_of(((row + 16 - k) % 16) * 256, 128)
+            modp[:, pl.ds(lo, 128)] = g[0:8]
+            modp[:, pl.ds(pl.multiple_of(lo + 128, 128), 128)] = g[8:16]
         shares, gains = [], []
         for b in range(3):
-            col_b = jnp.sum(jnp.where(lane1 == b, both, 0.0), axis=1, keepdims=True) / 16384.0
+            chosen = jnp.where((lane1 == b) | (lane1 == b + 3), first, 0.0)
+            chosen = chosen + jnp.where(lane1 == b, second, 0.0)
+            col_b = jnp.sum(chosen, axis=1, keepdims=True) / 16384.0
             centre = col_b[0:4]
             gain = lax.rsqrt(col_b[4:8] - centre * centre + 1e-05)
             shares.append(jnp.concatenate([centre] * 4, axis=0))
@@ -447,17 +495,15 @@
             go(tag + "1")
             go(tag + "2")
 
+        kstep(1, 1)
+        qkv(0)
+        kstep(1, 2)
         both_kinds(fwd, "A")
         for g in (1, 2):
             both_kinds(begin, f"B{g}")
-        go("O")
-        kstep(1, 1)
-        qkv(0)
-        kstep(1, 2)
         qkv(1)
         kstep(2, 0)
         go("C1_0")
-        both_kinds(fwd, "B0")
         qkv(2)
         kstep(2, 1)
         go("C1_1")
@@ -466,6 +512,7 @@
         attend(0, False)
         kstep(2, 2)
         go("C1_2")
+        both_kinds(fwd, "B0")
         both_kinds(done, "A")
         both_kinds(begin, "B3")
         got("C0_1")
@@ -473,78 +520,93 @@
         kstep(3, 0)
         attend(1, False)
         kstep(3, 1)
+        go("S0a")
         got("C0_2")
         got("C1_2")
-        got("O")
-        go("OS0")
         attend(2, False)
         kstep(3, 2)
         kstep(4, 0)
         go("C2_0")
-        both_kinds(fwd, "B1")
         kstep(4, 1)
         go("C2_1")
+        got("O")
+        go("OZ")
+        go("OS0")
         got("C2_0")
         attend(0, True)
         go("X0")
         kstep(4, 2)
         go("C2_2")
-        go("OZ")
+        both_kinds(fwd, "B1")
         got("C2_1")
         attend(1, True)
         go("X1")
         both_kinds(done, "B0")
-        go("S0")
+        go("S0b")
+        go("S1a")
         got("C2_2")
         attend(2, True)
         go("X2")
         both_kinds(fwd, "B2")
+        go("S2a")
+        c_ow.wait()
+        project_own(0)
+        project_own(1)
         got("OZ")
         go("OS1")
-        c_ow.wait()
+        project_own(2)
         got("OS0")
         got("X0")
         got("OS1")
         project(0)
-        both_kinds(fwd, "B3")
-        go("S3m")
-        go("S3e")
         got("X1")
         project(1)
+        both_kinds(fwd, "B3")
+        go("S3a")
         got("X2")
         project(2)
-        got("S0")
-        feed(0, 1)
+        got("S0a")
+        got("S1a")
+        feed(0, 2)
         both_kinds(done, "B1")
-        go("S1")
+        go("S1b")
         both_kinds(done, "B2")
-        go("S2")
-        got("S1")
-        feed(768, 2)
+        go("S2b")
+        got("S2a")
+        got("S3a")
+        feed(1536, 2)
         both_kinds(done, "B3")
-        go("S3mz")
-        go("S3ez")
-        got("S2")
-        feed(2304, 1)
-        got("S3m")
+        go("S3b")
+        got("S0b")
+        got("S1b")
         feed(3072, 1)
-        got("S3e")
-        got("S3mz")
-        got("S3ez")
+        got("S2b")
+        got("S3b")
         feed(3840, 1)
-        for b in range(3):
-            r = pl.ds(b * 128, 128)
-            out_ref[r, :] = (mid[r, :].astype(f32) + modrow(b, 5) * acc[r, :]).astype(bf)
+
+        def finish():
+            for b in range(3):
+                r = pl.ds(b * 128, 128)
+                outb[r, :] = (mid[r, :].astype(f32) + modrow(b, 5) * acc[r, :]).astype(bf)
+            for b in range(3):
+                r = pl.ds(b * 128, 128)
+                load(outb.at[r, :], out_ref.at[r, :])
+            for c in loads[-3:]:
+                c.wait()
+
+        finish()
         for c in copies.values():
             c.wait_send()
+        all15("M").wait_send()
+        all15("G").wait_send()
 
     any_spec = pl.BlockSpec(memory_space=pl.ANY)
-    n_copies = 2 * 20 + 7 + 3 * 12 + 4 + 5 + 30
+    n_copies = 2 * 20 + 8 + 3 * 12 + 4 + 5 + 2
     return pl.pallas_call(
         kernel,
         out_shape=jax.ShapeDtypeStruct((384, D), bf),
         in_specs=[pl.BlockSpec(memory_space=pltpu.SMEM)] * 2 + [any_spec] * 12,
-        out_specs=pl.BlockSpec(memory_space=pltpu.VMEM),
+        out_specs=any_spec,
         scratch_shapes=[
             pltpu.VMEM((3, 2, 3, 4, 4, 32), f32),
             pltpu.VMEM((3, 4, 16, 64), f32),
@@ -559,9 +621,10 @@
             pltpu.VMEM((3, 256, 640), f32),
             pltpu.VMEM((3, 256, 128), f32),
             pltpu.VMEM((8, 4096), f32),
-            pltpu.VMEM((16, 8, 256), f32),
-            pltpu.VMEM((8, 384), f32),
-            pltpu.VMEM((16, 8, 384), f32),
+            pltpu.VMEM((16, 2048), bf),
+            pltpu.VMEM((16, 16, 128), bf),
+            pltpu.VMEM((32, 128), bf),
+            pltpu.VMEM((16, 32, 128), bf),
             pltpu.VMEM((8, 4096), f32),
             pltpu.VMEM((3, 4, 16, 64), f32),
             pltpu.VMEM((3, 4, 2, 32, D), bf),
@@ -575,12 +638,13 @@
             pltpu.VMEM((384, D), bf),
             pltpu.VMEM((384, D), bf),
             pltpu.VMEM((384, D), f32),
+            pltpu.VMEM((384, D), bf),
             pltpu.SemaphoreType.DMA((n_copies,)),
             pltpu.SemaphoreType.DMA((n_copies,)),
-            pltpu.SemaphoreType.DMA((14,)),
+            pltpu.SemaphoreType.DMA((18,)),
         ],
         compiler_params=pltpu.CompilerParams(
-            collective_id=0, has_side_effects=True, vmem_limit_bytes=64_000_000
+            collective_id=0, has_side_effects=True, vmem_limit_bytes=58_000_000
         ),
     )(t_index, labels, x_lo, noise, embed, tw1, tw2, table, ada, stale, wqkv, ow, fc1, fc2)
 

time: 96.7 us -> 90.1 us (0.932)
  Pallas kernels: 94.4 us -> 87.8 us
    pallas_call x1, Pallas kernels: 94.4 us -> 87.8 us  [fused_block(): pl.pallas_call(kernel, out_shape=jax.ShapeDtypeStruct((384, D), bf), in_s...]
where the time goes in v4:
time: 90.1 us; the launch traced here: 90 us
  Pallas kernels  87.8 us (97%)
  local copies, waits for them, and re-layouts  2.17 us (2%)
    pallas_call x1, Pallas kernels, fused_block(): pl.pallas_call(kernel, out_shape=jax.ShapeDtypeStruct((384, D), bf), in_s...  87.8 us
    unnamed x1, local copies, waits for them, and re-layouts  2.17 us

profile of v4, /device:TPU:1, one launch (start us, length us, event | category | flops | bytes accessed | tf_op | source)
XLA Modules:
  0.0 90.0 jit_solution(8866388161280163529)
XLA Ops:
  0.0 87.8 %shard_map.136 = bf16[384,1152]{1,0:T(8,128)(2,1)} custom-call(s32[3]{0:T(128)} %t_s.1, s32[3]{0:T(128)} %label_s.1, f32[3,4,4,32]{3,2,1,0:T(4,128)} %bitcast.17, f32[3,4,16,64]{3,2,1,0:T(8,128)} %bitcast.16, f32[16,1152]{1,0:T(8,128)} %embed_h.1, bf16[256,1152]{1,0:T(8,128)(2,1)} %tw1_h.1, bf16[72,1152]{1,0:T(8,128)(2,1)} %bitcast.14, ...), custom_call_target="tpu_custom_call" | custom-call | tf_op jit(solution)/shard_map/pallas_call | solution.py:605
  87.8 2.2 %copy.16 = bf16[3,4,32,1152]{3,2,1,0:T(8,128)(2,1)} copy(bf16[3,4,32,1152]{3,2,1,0:T(8,128)(2,1)} %bitcast.11) | data formatting | bytes 1769472

commit v5 on v4

--- a/solution.py
+++ b/solution.py
@@ -513,12 +513,12 @@
         kstep(2, 2)
         go("C1_2")
         both_kinds(fwd, "B0")
-        both_kinds(done, "A")
-        both_kinds(begin, "B3")
         got("C0_1")
         got("C1_1")
         kstep(3, 0)
         attend(1, False)
+        both_kinds(done, "A")
+        both_kinds(begin, "B3")
         kstep(3, 1)
         go("S0a")
         got("C0_2")
@@ -548,12 +548,12 @@
         attend(2, True)
         go("X2")
         both_kinds(fwd, "B2")
-        go("S2a")
         c_ow.wait()
         project_own(0)
-        project_own(1)
         got("OZ")
         go("OS1")
+        go("S2a")
+        project_own(1)
         project_own(2)
         got("OS0")
         got("X0")

time: 90.1 us -> 90.1 us (level)
  no operation moved by 1% of the time
where the time goes in v5:
time: 90.1 us; the launch traced here: 90 us
  Pallas kernels  87.8 us (97%)
  local copies, waits for them, and re-layouts  2.17 us (2%)
    pallas_call x1, Pallas kernels, fused_block(): pl.pallas_call(kernel, out_shape=jax.ShapeDtypeStruct((384, D), bf), in_s...  87.8 us
    unnamed x1, local copies, waits for them, and re-layouts  2.17 us

profile of v5, /device:TPU:1, one launch (start us, length us, event | category | flops | bytes accessed | tf_op | source)
XLA Modules:
  0.0 90.0 jit_solution(2285605396108871986)
XLA Ops:
  0.0 87.8 %shard_map.136 = bf16[384,1152]{1,0:T(8,128)(2,1)} custom-call(s32[3]{0:T(128)} %t_s.1, s32[3]{0:T(128)} %label_s.1, f32[3,4,4,32]{3,2,1,0:T(4,128)} %bitcast.17, f32[3,4,16,64]{3,2,1,0:T(8,128)} %bitcast.16, f32[16,1152]{1,0:T(8,128)} %embed_h.1, bf16[256,1152]{1,0:T(8,128)(2,1)} %tw1_h.1, bf16[72,1152]{1,0:T(8,128)(2,1)} %bitcast.14, ...), custom_call_target="tpu_custom_call" | custom-call | tf_op jit(solution)/shard_map/pallas_call | solution.py:605
  87.8 2.2 %copy.16 = bf16[3,4,32,1152]{3,2,1,0:T(8,128)(2,1)} copy(bf16[3,4,32,1152]{3,2,1,0:T(8,128)(2,1)} %bitcast.11) | data formatting | bytes 1769472

commit v6 on v4

--- a/solution.py
+++ b/solution.py
@@ -18,7 +18,7 @@
     bf, f32 = jnp.bfloat16, jnp.float32
     NKEY = 256 + 15 * 64
     HID = 4608
-    UNROLL = 2
+    UNROLL = 4
     EARLY = 256 + 9 * 64
 
     def kernel(

time: 90.1 us -> 90.1 us (level)
  no operation moved by 1% of the time
where the time goes in v6:
time: 90.1 us; the launch traced here: 90 us
  Pallas kernels  87.8 us (97%)
  local copies, waits for them, and re-layouts  2.17 us (2%)
    pallas_call x1, Pallas kernels, fused_block(): pl.pallas_call(kernel, out_shape=jax.ShapeDtypeStruct((384, D), bf), in_s...  87.8 us
    unnamed x1, local copies, waits for them, and re-layouts  2.17 us

profile of v6, /device:TPU:1, one launch (start us, length us, event | category | flops | bytes accessed | tf_op | source)
XLA Modules:
  0.0 90.0 jit_solution(10756121765708948205)
XLA Ops:
  0.0 87.8 %shard_map.136 = bf16[384,1152]{1,0:T(8,128)(2,1)} custom-call(s32[3]{0:T(128)} %t_s.1, s32[3]{0:T(128)} %label_s.1, f32[3,4,4,32]{3,2,1,0:T(4,128)} %bitcast.17, f32[3,4,16,64]{3,2,1,0:T(8,128)} %bitcast.16, f32[16,1152]{1,0:T(8,128)} %embed_h.1, bf16[256,1152]{1,0:T(8,128)(2,1)} %tw1_h.1, bf16[72,1152]{1,0:T(8,128)(2,1)} %bitcast.14, ...), custom_call_target="tpu_custom_call" | custom-call | tf_op jit(solution)/shard_map/pallas_call | solution.py:605
  87.8 2.2 %copy.16 = bf16[3,4,32,1152]{3,2,1,0:T(8,128)(2,1)} copy(bf16[3,4,32,1152]{3,2,1,0:T(8,128)(2,1)} %bitcast.11) | data formatting | bytes 1769472
